TPU v7x, 256 devices: a whole 4x4x8 slice. The times are simulated.
256 devices in a mesh: seq: 16 (over z, x_lo), img: 8 (over y, x_hi), fsdp: 2 (over core).
Axes of the slice: x: 4 (x_hi: 2, x_lo: 2; x = x_hi * 2 + x_lo), y: 4, z: 8, core: 2. Of those that a mesh axis runs over, the one named last changes fastest.
Arguments:
- vision_feats: bfloat16 [8, 2304, 1024], P('img', ('seq', 'fsdp')), may hold values from -6 to 6
- ln_gain: float32 [1024], replicated, may hold values from 0.5 to 1.5
- ln_bias: float32 [1024], replicated, may hold values from -3 to 3
- w_in: bfloat16 [1024, 4096], P('fsdp', 'seq'), may hold values from -0.1875 to 0.1875
- b_in: float32 [4096], P('seq'), may hold values from -3 to 3
- w_out: bfloat16 [4096, 4096], P('seq', 'fsdp'), may hold values from -0.09375 to 0.09375
- lm_grad: bfloat16 [8, 4096, 4096], P('img', 'seq', 'fsdp'), may hold values from -0.079589844 to 0.079589844
- image_counts: int32 [8, 2], P('img'), may hold values from 1 to 3, as said below
- token_pos: int32 [8, 2304], P('img'), may hold values from 0 to 2047, as said below
Outputs:
- w_in_grad: float32 [1024, 4096], P(('img', 'fsdp'), 'seq')
- b_in_grad: float32 [4096], replicated
- w_out_grad: float32 [4096, 4096], P(('seq', 'img'), 'fsdp')
- b_out_grad: float32 [4096], replicated
- ln_gain_grad: float32 [1024], replicated
- ln_bias_grad: float32 [1024], replicated
Inputs may be any that keep to these rules, and one draw needn't show every extreme that they name: `image_counts`: in each group the 2 samples hold 4 images together, each sample one or more. `token_pos`: each image's 576 tokens take consecutive positions of its sample's sequence in order; a sample's images come in order without intersection, and images are numbered sample by sample as image_counts gives.
All inputs are finite; a program needn't handle non-finite values.
Results may differ from a plain program's by a relative error of at most 0.0047.
Values may be sent and summed in bfloat16 or wider, within the bound.
No kernel may reach another device: no remote copies, remote signals or barrier semaphores. Data moves between devices by JAX's collectives and lax.ppermute only.
A program may use at most 128 MiB of HBM per device.

v0:
```python
import jax
import jax.numpy as jnp
from jax import lax
from jax.experimental import pallas as pl
from jax.experimental.pallas import tpu as pltpu
from jax.sharding import Mesh
from jax.sharding import PartitionSpec as P

PATCH = 576
LEN = 2048
SEQ = ("z", "xl")
IMG = ("y", "xh")
PLANE = ("xl", "y", "xh")


def gelu_parts(preact):
    cumul = 0.5 * (1.0 + lax.erf(preact * 0.7071067811865476))
    density = jnp.exp(-0.5 * preact * preact) * 0.3989422804014327
    return (preact * cumul, cumul + preact * density)


def contract(left, right, left_dim, right_dim):
    return lax.dot_general(
        left, right, (((left_dim,), (right_dim,)), ((), ())), preferred_element_type=jnp.float32
    )


def swap(array, axis):
    return lax.ppermute(array, axis, [(0, 1), (1, 0)])


def in_axis_order(own, other, axis):
    first = lax.axis_index(axis) == 0
    return jnp.where(first, own, other), jnp.where(first, other, own)


def along_z(array, shift):
    count = lax.axis_size("z")
    return lax.ppermute(array, "z", [(i, (i + shift) % count) for i in range(count)])


def gate(*values):
    return lax.optimization_barrier(values)


def whole(shape):
    return pl.BlockSpec(shape, lambda *_: (0,) * len(shape))


def summed_product(left, blocks):
    rows, width = blocks[0].shape
    tile = width // 2

    def kernel(left_ref, *refs):
        right = jnp.concatenate([ref[...] for ref in refs[:-1]], axis=0)
        total = jnp.dot(left_ref[...], right, preferred_element_type=jnp.float32)
        refs[-1][...] = total.astype(jnp.bfloat16)

    flops = 2 * left.shape[0] * left.shape[1] * width
    return pl.pallas_call(
        kernel,
        grid=(width // tile,),
        in_specs=[whole(left.shape)]
        + [pl.BlockSpec((rows, tile), lambda j: (0, j)) for _ in blocks],
        out_specs=pl.BlockSpec((left.shape[0], tile), lambda j: (0, j)),
        out_shape=jax.ShapeDtypeStruct((left.shape[0], width), jnp.bfloat16),
        cost_estimate=pl.CostEstimate(
            flops=flops,
            bytes_accessed=2 * (left.size + 2 * blocks[0].size * len(blocks)),
            transcendentals=0,
        ),
        name="summed_product",
    )(left, *blocks)


def hidden_products(weights, place, first, second):
    rows, width = first[0].shape
    count = len(first)
    hidden = weights[0].shape[0]

    def kernel(place_ref, own_ref, other_ref, *refs):
        total_ref, rounded_ref = refs[2 * count :]
        spots = (place_ref[0], 1 - place_ref[0])
        for i in range(count):
            block = jnp.concatenate([refs[i][...], refs[count + i][...]], axis=1)
            for ref, spot in zip((own_ref, other_ref), spots):
                total = contract(ref[...], block, 1, 1)
                here = pl.ds(pl.multiple_of(spot * hidden, hidden), hidden)
                total_ref[here, i * rows : (i + 1) * rows] = total
                rounded_ref[here, i * rows : (i + 1) * rows] = total.astype(jnp.bfloat16)

    out = (2 * hidden, count * rows)
    return pl.pallas_call(
        kernel,
        grid_spec=pltpu.PrefetchScalarGridSpec(
            num_scalar_prefetch=1,
            grid=(1,),
            in_specs=[whole(weights[0].shape)] * 2 + [whole(first[0].shape)] * (2 * count),
            out_specs=[whole(out), whole(out)],
        ),
        out_shape=[jax.ShapeDtypeStruct(out, jnp.float32), jax.ShapeDtypeStruct(out, jnp.bfloat16)],
        cost_estimate=pl.CostEstimate(
            flops=8 * count * rows * width * hidden,
            bytes_accessed=4 * count * rows * width,
            transcendentals=0,
        ),
        name="hidden_products",
    )(place, *weights, *first, *second)


def forward(
    seen, held_pos, bases, window_starts, image_starts, w_turned, b_column, gain, bias, core, rows, piece
):
    count = bases.shape[0]
    _, window, feats = seen.shape
    window = 2 * window
    hidden = w_turned.shape[0]
    images = image_starts.shape[0]

    def own_half(array, core):
        lane = lax.broadcasted_iota(jnp.int32, (rows, 2 * piece), 1)
        first = core == 0
        kept = (lane < piece) == first
        held = []
        for i in range(0, feats, 4 * piece):
            left, right = array[:, i : i + 2 * piece], array[:, i + 2 * piece : i + 4 * piece]
            turned = pltpu.roll(jnp.where(first, right, left), piece, 1)
            held.append(jnp.where(kept, jnp.where(first, left, right), turned))
        return jnp.concatenate(held, axis=1)

    def kernel(base_ref, window_ref, image_ref, core_ref, seen_ref, pos_ref, w_ref, b_ref, gain_ref, bias_ref, own_gain_ref, own_bias_ref,
               in_ref, normed_ref, hidden_ref, slope_ref):
        step = pl.program_id(0)
        base = base_ref[step]
        begin = window_ref[step]
        own = base + lax.broadcasted_iota(jnp.int32, (rows, window), 0)
        select = (own == pos_ref[begin]).astype(jnp.float32).astype(jnp.bfloat16)
        held = seen_ref[pl.ds(begin, 2)].reshape(window, feats)
        placed = jnp.dot(select, held, preferred_element_type=jnp.float32)
        mean = jnp.mean(placed, axis=1, keepdims=True)
        centred = placed - mean
        var = jnp.mean(centred * centred, axis=1, keepdims=True)
        normed = centred * lax.rsqrt(var + 1e-05)
        normed_in = (normed * gain_ref[...] + bias_ref[...]).astype(jnp.bfloat16)
        own_normed = own_half(normed, core_ref[0])
        in_ref[...] = (own_normed * own_gain_ref[...] + own_bias_ref[...]).astype(jnp.bfloat16)
        normed_ref[...] = own_normed.astype(jnp.bfloat16)
        preact = contract(w_ref[...], normed_in, 1, 1) + b_ref[...]
        activ, slope = gelu_parts(preact)
        column = base + lax.broadcasted_iota(jnp.int32, (1, rows), 1)
        mask = jnp.zeros((1, rows), jnp.float32)
        for i in range(images):
            start = image_ref[i]
            inside = (column >= start) & (column < start + PATCH)
            mask = jnp.where(inside, 1.0, mask)
        hidden_ref[...] = (activ * mask).astype(jnp.bfloat16)
        slope_ref[...] = slope * mask

    positions = count * rows
    return pl.pallas_call(
        kernel,
        grid_spec=pltpu.PrefetchScalarGridSpec(
            num_scalar_prefetch=4,
            grid=(count,),
            in_specs=[
                whole(seen.shape),
                whole(held_pos.shape),
                whole(w_turned.shape),
                whole((hidden, 1)),
                whole((1, feats)),
                whole((1, feats)),
                whole((1, feats // 2)),
                whole((1, feats // 2)),
            ],
            out_specs=[
                pl.BlockSpec((rows, feats // 2), lambda i, *_: (i, 0)),
                pl.BlockSpec((rows, feats // 2), lambda i, *_: (i, 0)),
                pl.BlockSpec((hidden, rows), lambda i, *_: (0, i)),
                pl.BlockSpec((hidden, rows), lambda i, *_: (0, i)),
            ],
        ),
        out_shape=[
            jax.ShapeDtypeStruct((positions, feats // 2), jnp.bfloat16),
            jax.ShapeDtypeStruct((positions, feats // 2), jnp.bfloat16),
            jax.ShapeDtypeStruct((hidden, positions), jnp.bfloat16),
            jax.ShapeDtypeStruct((hidden, positions), jnp.float32),
        ],
        cost_estimate=pl.CostEstimate(
            flops=2 * positions * feats * (window + hidden),
            bytes_accessed=20 * positions * hidden,
            transcendentals=2 * positions * hidden,
        ),
        name="forward",
    )(bases, window_starts, image_starts, core, seen, held_pos, w_turned, b_column, gain[0], bias[0], gain[1], bias[1])


TILE = 256


def preact_grads(parts, others, slope_ref, held_ref, groups, rows):
    at = 0
    for part, other, group in zip(parts, others, groups):
        for i, block in enumerate(group):
            here = slice(i * rows, (i + 1) * rows)
            total = part[:, here] + other[:, here].astype(jnp.float32)
            total = total * slope_ref[:, block * rows : (block + 1) * rows]
            held_ref[:, at * rows : (at + 1) * rows] = total.astype(jnp.bfloat16)
            at += 1


def of_groups(ref, groups, rows):
    return jnp.concatenate(
        [ref[i * rows : (i + 1) * rows, :] for group in groups for i in group], axis=0
    )


def input_products(parts, others, slope, normed_in, normed, groups, rows):
    count = len(groups)
    hidden = slope.shape[0]
    held = rows * sum(len(group) for group in groups)
    positions, feats = normed_in.shape

    def kernel(*refs):
        parts, others = refs[:count], refs[count : 2 * count]
        slope_ref, in_ref, normed_ref, w_out, g_out, b_out, held_ref = refs[2 * count :]

        @pl.when(pl.program_id(0) == 0)
        def _():
            preact_grads(parts, others, slope_ref, held_ref, groups, rows)
            ones = jnp.ones((8, held), jnp.bfloat16)
            b_out[...] = contract(ones, held_ref[...], 1, 1)

        grads = held_ref[...]
        w_out[...] = jnp.dot(
            grads, of_groups(in_ref, groups, rows), preferred_element_type=jnp.float32
        )
        g_out[...] = jnp.dot(
            grads, of_groups(normed_ref, groups, rows), preferred_element_type=jnp.float32
        )

    column = pl.BlockSpec((positions, TILE), lambda j: (0, j))
    tile = pl.BlockSpec((hidden, TILE), lambda j: (0, j))
    return pl.pallas_call(
        kernel,
        grid=(feats // TILE,),
        in_specs=[whole(a.shape) for a in (*parts, *others)] + [whole(slope.shape), column, column],
        out_specs=[tile, tile, whole((8, hidden))],
        out_shape=[
            jax.ShapeDtypeStruct((hidden, feats), jnp.float32),
            jax.ShapeDtypeStruct((hidden, feats), jnp.float32),
            jax.ShapeDtypeStruct((8, hidden), jnp.float32),
        ],
        scratch_shapes=[pltpu.VMEM((hidden, held), jnp.bfloat16)],
        cost_estimate=pl.CostEstimate(
            flops=4 * held * hidden * feats, bytes_accessed=8 * positions * feats, transcendentals=0
        ),
        name="input_products",
    )(*parts, *others, slope, normed_in, normed)


def input_pieces(part, other, slope, normed_in, normed, before, w_own, out_rows, rows, at, images):
    hidden, held = part.shape
    own_feats = normed_in.shape[1]
    piece = own_feats // images
    width = hidden // 2
    steps = own_feats // TILE
    per_step = images // steps
    b_rows = hidden // TILE
    total_rows = 2 * steps + b_rows + out_rows.shape[0]
    padded = -(-total_rows // 8) * 8

    def kernel(part_ref, other_ref, slope_ref, in_ref, normed_ref, w_before, g_before, b_before,
               w_ref, rows_ref, sent_ref, held_ref, vector_ref, column_ref):
        step = pl.program_id(0)

        @pl.when(step == 0)
        def _():
            preact_grads([part_ref], [other_ref], slope_ref, held_ref, [range(held // rows)], rows)
            ones = jnp.ones((8, held), jnp.bfloat16)
            sums = contract(ones, held_ref[...], 1, 1) + b_before[...]
            vector_ref[...] = jnp.zeros_like(vector_ref)
            for i in range(b_rows):
                vector_ref[2 * steps + i : 2 * steps + i + 1, :] = sums[
                    0:1, i * TILE : (i + 1) * TILE
                ]
            first = 2 * steps + b_rows
            vector_ref[first : first + rows_ref.shape[0], :] = rows_ref[...]
            column_ref[...] = jnp.broadcast_to(sums[0:1, :], (128, hidden)).T

        grads = held_ref[...]
        w_grad = w_before[...] + jnp.dot(grads, in_ref[...], preferred_element_type=jnp.float32)
        g_grad = g_before[...] + jnp.dot(grads, normed_ref[...], preferred_element_type=jnp.float32)
        turned = w_grad.T.astype(jnp.bfloat16)
        for i in range(per_step):
            for half in range(2):
                sent_ref[half * images + step * per_step + i, 0:piece, :] = turned[
                    i * piece : (i + 1) * piece, half * width : (half + 1) * width
                ]
        weights = w_ref[...].astype(jnp.float32)
        column = jnp.concatenate([column_ref[...]] * (TILE // 128), axis=1)
        vector_ref[pl.ds(step, 1), :] = jnp.sum(g_grad * weights, axis=0, keepdims=True)
        vector_ref[pl.ds(steps + step, 1), :] = jnp.sum(column * weights, axis=0, keepdims=True)

        @pl.when(step == steps - 1)
        def _():
            vectors = vector_ref[...]
            high = vectors.astype(jnp.bfloat16).astype(jnp.float32)
            both = jnp.concatenate([high, vectors - high], axis=0).astype(jnp.bfloat16)
            for i in range(2 * images):
                sent_ref[i, piece : piece + 2 * padded, :] = both

    column = pl.BlockSpec((held, TILE), lambda j: (at, j))
    tile = pl.BlockSpec((hidden, TILE), lambda j: (0, j))
    sent = (2 * images, piece + 2 * padded, width)
    return pl.pallas_call(
        kernel,
        grid=(steps,),
        in_specs=[
            whole(part.shape),
            whole(part.shape),
            pl.BlockSpec((hidden, held), lambda j: (0, at)),
            column,
            column,
            tile,
            tile,
            whole((8, hidden)),
            tile,
            whole(out_rows.shape),
        ],
        out_specs=whole(sent),
        scratch_shapes=[
            pltpu.VMEM((hidden, held), jnp.bfloat16),
            pltpu.VMEM((padded, TILE), jnp.float32),
            pltpu.VMEM((hidden, 128), jnp.float32),
        ],
        out_shape=jax.ShapeDtypeStruct(sent, jnp.bfloat16),
        cost_estimate=pl.CostEstimate(
            flops=4 * held * hidden * own_feats, bytes_accessed=8 * held * own_feats, transcendentals=0
        ),
        name="input_pieces",
    )(part, other, slope, normed_in, normed, *before, w_own, out_rows)


def split_terms(vector):
    high = vector.astype(jnp.bfloat16)
    low = (vector - high.astype(jnp.float32)).astype(jnp.bfloat16)
    return high, low


def one_step(vision_feats, ln_gain, ln_bias, w_in, b_in, w_out, lm_grad, image_counts, token_pos):
    z_count = lax.axis_size("z")
    z = lax.axis_index("z")
    xl = lax.axis_index("xl")
    core = lax.axis_index("c")
    vision = vision_feats[0]
    lm = lm_grad[0]
    rows, half_width = lm.shape
    feats = vision.shape[1]
    quarter = half_width // 2
    counts = image_counts[0]
    positions = token_pos[0]
    tokens = positions.shape[0]
    image_index = jnp.arange(tokens, dtype=jnp.int32) // PATCH
    abs_pos = jnp.where(image_index >= counts[0], LEN, 0) + positions
    copies = jnp.broadcast_to(vision, (z_count, *vision.shape))
    seen = lax.all_to_all(copies, "z", 0, 0, tiled=True)
    low, high = [None] * z_count, [None] * z_count
    low[0], high[0] = lm[:, :quarter], lm[:, quarter:]
    low[7], low[1] = along_z(low[0], 1), along_z(low[0], -1)
    high[7], high[1] = along_z(high[0], 1), along_z(high[0], -1)
    w_out_other = swap(w_out, "xl")
    terms = split_terms(b_in)
    third = (b_in - terms[0].astype(jnp.float32) - terms[1].astype(jnp.float32)).astype(jnp.bfloat16)
    w_in_other = swap(w_in, "c")
    w_first, w_second = in_axis_order(w_in, w_in_other, "c")
    packed = jnp.concatenate(
        [w_first, w_second, jnp.stack([*terms, third]), jnp.zeros((5, b_in.shape[0]), jnp.bfloat16)]
    )
    packed_other = swap(packed, "xl")
    hidden_width = 2 * w_out.shape[0]
    plane_count = lax.axis_size(PLANE)
    img_count = lax.axis_size(IMG)
    piece = feats // (img_count * 2)
    packed = jnp.concatenate(in_axis_order(packed, packed_other, "xl"), axis=1)
    w_turned = packed[:feats].T
    w_own = packed[:feats].reshape(img_count, 2, piece, hidden_width)
    w_own = lax.dynamic_index_in_dim(w_own, core, 1, False).reshape(feats // 2, hidden_width).T
    b_column = jnp.sum(packed[feats : feats + 3].astype(jnp.float32), axis=0)[:, None]
    block_of = lax.rem(z + jnp.arange(z_count, dtype=jnp.int32), z_count)
    bases = (2 * block_of + xl) * rows
    image_starts = abs_pos[::PATCH]
    first_token = jnp.sum((abs_pos[None, :] < bases[:, None]).astype(jnp.int32), axis=1)
    of_z = tokens // z_count
    window_starts = jnp.minimum(first_token // of_z, z_count - 2)
    held_pos = abs_pos.reshape(z_count, 2, 2, of_z // 4)
    held_pos = jnp.where(xl == 0, held_pos, held_pos[:, ::-1])
    held_pos = jnp.where(core == 0, held_pos, held_pos[:, :, ::-1])
    held_pos = held_pos.transpose(0, 2, 1, 3).reshape(z_count, 1, of_z)
    own_pos = bases[0] + jnp.arange(rows, dtype=jnp.int32)
    inside = (own_pos[:, None] >= image_starts) & (own_pos[:, None] < image_starts + PATCH)
    mask = jnp.any(inside, axis=1).astype(jnp.bfloat16)
    out_part = jnp.dot(mask[None, :], lm, preferred_element_type=jnp.float32).reshape(-1, TILE)
    held_pos = jnp.concatenate([held_pos[:-1], held_pos[1:]], axis=2)

    def own_part(vector):
        parts = vector.reshape(img_count, 2, piece)
        return lax.dynamic_index_in_dim(parts, core, 1, False).reshape(1, -1)

    seen, w_turned, w_own, b_column, out_part, held_pos = gate(
        seen, w_turned, w_own, b_column, out_part, held_pos
    )
    seen_other = swap(seen, "xl")
    low[7], low[1] = gate(low[7], low[1])
    low[6], low[2] = along_z(low[7], 1), along_z(low[1], -1)
    high[7], high[1] = gate(high[7], high[1])
    high[6], high[2] = along_z(high[7], 1), along_z(high[1], -1)
    weights, place = (w_out, w_out_other), xl.reshape(1)

    def products(blocks):
        return hidden_products(weights, place, [low[i] for i in blocks], [high[i] for i in blocks])

    groups = [(7, 0, 1), (6, 2), (5, 3)]
    parts, others = [None] * 3, [None] * 3
    parts[0], rounded = products(groups[0])
    parts[0], rounded, seen_other = gate(parts[0], rounded, seen_other)
    seen = jnp.stack([seen, seen_other], axis=1)
    seen_other = swap(seen, "c")
    others[0] = swap(rounded, "c")
    low[6], low[2], rounded = gate(low[6], low[2], rounded)
    low[5], low[3] = along_z(low[6], 1), along_z(low[2], -1)
    seen = jnp.stack([seen, seen_other], axis=1).reshape(z_count, of_z, feats)
    normed_in, normed, hidden, slope = forward(
        seen,
        held_pos,
        bases,
        window_starts,
        image_starts,
        w_turned,
        b_column,
        (ln_gain[None, :], own_part(ln_gain)),
        (ln_bias[None, :], own_part(ln_bias)),
        core.reshape(1),
        rows,
        piece,
    )
    high[6], high[2], hidden, others[0] = gate(high[6], high[2], hidden, others[0])
    high[5], high[3] = along_z(high[6], 1), along_z(high[2], -1)
    low[5], low[3], hidden = gate(low[5], low[3], hidden)
    low[4] = along_z(low[5], 1)
    parts[1], rounded = products(groups[1])
    others[1] = swap(rounded, "c")
    high[5], high[3], parts[1] = gate(high[5], high[3], parts[1])
    high[4] = along_z(high[3], -1)
    parts[2], rounded = products(groups[2])
    others[2] = swap(rounded, "c")
    low[4], hidden, parts[2], rounded = gate(low[4], hidden, parts[2], rounded)
    low_product = summed_product(hidden, low)
    low_product, normed_in, normed, slope = gate(low_product, normed_in, normed, slope)
    low_moved = lax.all_to_all(low_product, PLANE, 0, 0, tiled=True)
    before = input_products(parts, others, slope, normed_in, normed, groups, rows)
    high[4], *before = gate(high[4], *before)
    part, rounded = products((4,))
    other = swap(rounded, "c")
    high_product = summed_product(hidden, high)
    sent = input_pieces(
        part, other, slope, normed_in, normed, before, w_own, out_part, rows, 4, img_count
    )
    sent, low_moved = gate(sent, low_moved)
    moved = lax.all_to_all(sent, PLANE, 0, 0, tiled=True)
    moved, high_product = gate(moved, high_product)
    high_moved = lax.all_to_all(high_product, PLANE, 0, 0, tiled=True)
    summed = jnp.sum(moved.astype(jnp.float32), axis=0)
    w_in_grad = summed[:piece]
    padded = (summed.shape[0] - piece) // 2
    vectors = summed[piece : piece + padded] + summed[piece + padded :]
    line = feats // 2 // TILE
    b_lines = hidden_width // TILE
    out_lines = half_width // TILE
    b_own = vectors[2 * line : 2 * line + b_lines]
    b_full = jnp.where((jnp.arange(z_count) == z)[:, None, None], b_own[None], 0.0)
    vectors = jnp.concatenate(
        [
            vectors[: 2 * line],
            vectors[2 * line + b_lines : 2 * line + b_lines + out_lines],
            b_full.reshape(-1, TILE),
        ]
    )
    for shift in (1, 2, 4):
        moved = lax.ppermute(vectors, "z", [(i, i ^ shift) for i in range(z_count)])
        vectors = vectors + moved
    first, second = in_axis_order(vectors, swap(vectors, "c"), "c")

    def by_core(low_half, high_half):
        return jnp.stack([low_half.reshape(-1, piece), high_half.reshape(-1, piece)], 1).reshape(-1)

    gain_grad = by_core(first[:line], second[:line])
    bias_grad = by_core(first[line : 2 * line], second[line : 2 * line])
    out_end = 2 * line + out_lines
    b_out_grad = jnp.concatenate([first[2 * line : out_end], second[2 * line : out_end]]).reshape(-1)
    b_in_grad = first[out_end:].reshape(-1)

    def over_plane(array):
        return jnp.sum(array.reshape(plane_count, -1, quarter).astype(jnp.float32), axis=0)

    w_out_grad = jnp.concatenate([over_plane(low_moved), over_plane(high_moved)], axis=1)
    return (w_in_grad, b_in_grad, w_out_grad, b_out_grad, gain_grad, bias_grad)


def solution(mesh):
    finer = Mesh(
        mesh.devices.reshape(8, 2, 4, 2, mesh.shape["fsdp"]),
        ("z", "xl", "y", "xh", "c"),
    )
    placed = (
        P(IMG, ("z", "xl", "c"), None),
        P(),
        P(),
        P("c", SEQ),
        P(SEQ),
        P(SEQ, "c"),
        P(IMG, SEQ, "c"),
        P(IMG, None),
        P(IMG, None),
    )

    return jax.shard_map(
        one_step,
        mesh=finer,
        in_specs=placed,
        out_specs=(P(("y", "xh", "c"), SEQ), P(), P(("z", "xl", "y", "xh"), "c"), P(), P(), P()),
        check_vma=False,
    )
```

profile of v0, /device:TPU:1, one launch (start us, length us, event | category | flops | bytes accessed | tf_op | source)
XLA Modules:
  0.0 262.4 jit_solution(9605404793081772496)
XLA Ops:
  1.8 3.3 %collective-permute-start.7 = (bf16[512,256]{0,1:T(8,128)(2,1)S(1)}, bf16[512,256]{0,1:T(8,128)(2,1)S(1)}, u32[]{:S(2)}, u32[]{:S(2)}) collective-permute-start(bf16[512,256]{0,1:T(8,128)(2,1)S(1)} %copy.50), channel_id=1, source_target_pairs={{0,1},{1,0},{2,3},{3,2},{4,5},{5,4},{6,7},{7,6},{8,9},{9,8},{10,11... | collective-permute-start | bytes 786440 | tf_op jit(solution)/shard_map/ppermute | solution.py:29
  5.1 2.1 broadcast_in_dim.60
  7.2 6.6 %all-to-all-start = ((bf16[8,72,1024]{2,1,0:T(8,128)(2,1)}), bf16[8,72,1024]{2,1,0:T(8,128)(2,1)}, u32[]{:S(2)}, u32[]{:S(2)}) async-start(bf16[8,72,1024]{2,1,0:T(8,128)(2,1)} %broadcast_in_dim.60), calls=%async_computation | async-start | bytes 2359296 | tf_op jit(solution)/shard_map/all_to_all | solution.py:366
  14.9 1.5 collective-permute-start.1
  20.6 1.5 fusion.1
  23.4 28.2 %collective-permute-done.8 = bf16[1032,256]{1,0:T(8,128)(2,1)S(1)} collective-permute-done((bf16[1032,256]{1,0:T(8,128)(2,1)}, bf16[1032,256]{1,0:T(8,128)(2,1)S(1)}, u32[]{:S(2)}, u32[]{:S(2)}) %collective-permute-start.8) | collective-permute-done | bytes 528416 | tf_op jit(solution)/shard_map/ppermute | solution.py:29
  55.8 2.4 copy.58
  58.1 1.9 constant_dynamic-slice_fusion
  60.0 2.1 copy.59
  62.2 1.3 collective-permute-start.9
  63.5 1.5 collective-permute-start.2
  65.0 2.7 %collective-permute-start.6 = (bf16[256,1024]{1,0:T(8,128)(2,1)}, bf16[256,1024]{1,0:T(8,128)(2,1)S(1)}, u32[]{:S(2)}, u32[]{:S(2)}) collective-permute-start(bf16[256,1024]{1,0:T(8,128)(2,1)} %get-tuple-element.122.refs_4_.refs_0_), channel_id=1, source_target_pairs={{0,224},{32,0},{64,32},{96,64},{128,96},{160,128},{192,160},{224,1... | collective-permute-start | bytes 1572872 | tf_op jit(solution)/shard_map/ppermute | solution.py:39
  67.7 7.7 %collective-permute-done.2.refs_2_.refs_1_ = bf16[256,1024]{1,0:T(8,128)(2,1)} collective-permute-done((bf16[256,1024]{1,0:T(8,128)(2,1)}, bf16[256,1024]{1,0:T(8,128)(2,1)}, u32[]{:S(2)}, u32[]{:S(2)}) %collective-permute-start.2) | collective-permute-done | bytes 524320 | tf_op jit(solution)/shard_map/ppermute | solution.py:39
  75.4 2.6 collective-permute-done.5.refs_3_.refs_7_
  78.0 8.5 %collective-permute-done.6.refs_5_.refs_1_ = bf16[256,1024]{1,0:T(8,128)(2,1)S(1)} collective-permute-done((bf16[256,1024]{1,0:T(8,128)(2,1)}, bf16[256,1024]{1,0:T(8,128)(2,1)S(1)}, u32[]{:S(2)}, u32[]{:S(2)}) %collective-permute-start.6) | collective-permute-done | bytes 524320 | tf_op jit(solution)/shard_map/ppermute | solution.py:39
  88.4 5.9 %hidden_products.4 = (f32[512,768]{1,0:T(8,128)}, bf16[512,768]{1,0:T(8,128)(2,1)}) custom-call(s32[1]{0:T(128)} %bitcast.place_ref, bf16[256,2048]{1,0:T(8,128)(2,1)} %own_ref.7, bf16[256,2048]{1,0:T(8,128)(2,1)} %copy-done.1, bf16[256,1024]{1,0:T(8,128)(2,1)} %collective-permute-done.1.refs_0_.refs_7_, ...), custom_call_target="tpu_custom_call" | custom-call | flops 1610612736 | bytes 3145728 | tf_op jit(solution)/shard_map/hidden_products/pallas_call | solution.py:93
  94.2 3.0 %fusion.19 = (bf16[8,1,2,72,1024]{4,3,2,1,0:T(8,128)(2,1)S(1)}, bf16[8,2,72,1024]{3,2,1,0:T(8,128)(2,1)}) fusion(bf16[8,1,72,1024]{3,2,1,0:T(8,128)(2,1)S(1)} %bitcast.55, bf16[8,1,72,1024]{3,2,1,0:T(8,128)(2,1)} %bitcast.15), kind=kLoop, calls=%fused_computation.71 | loop fusion | flops 1179648 | bytes 7077888 | tf_op jit(solution)/shard_map/stack | solution.py:431
  97.2 2.7 %collective-permute-start.14 = (bf16[8,2,72,1024]{3,2,1,0:T(8,128)(2,1)}, bf16[8,2,72,1024]{3,2,1,0:T(8,128)(2,1)}, u32[]{:S(2)}, u32[]{:S(2)}) collective-permute-start(bf16[8,2,72,1024]{3,2,1,0:T(8,128)(2,1)} %get-tuple-element.119), channel_id=1, source_target_pairs={{0,1},{1,0},{2,3},{3,2},{4,5},{5,4},{6,7},{7,6},{8,9},{9,8},{10,11... | collective-permute-start | bytes 7077896 | tf_op jit(solution)/shard_map/ppermute | solution.py:29
  101.1 1.5 collective-permute-start.4
  108.7 6.4 %collective-permute-done.3.refs_0_.refs_6_ = bf16[256,1024]{1,0:T(8,128)(2,1)} collective-permute-done((bf16[256,1024]{1,0:T(8,128)(2,1)}, bf16[256,1024]{1,0:T(8,128)(2,1)}, u32[]{:S(2)}, u32[]{:S(2)}) %collective-permute-start.3) | collective-permute-done | bytes 524320 | tf_op jit(solution)/shard_map/ppermute | solution.py:39
  115.0 1.4 collective-permute-start.13
  116.5 1.7 collective-permute-start.10
  119.1 4.3 %pad_maximum_fusion = bf16[8,2,2,72,1024]{4,3,2,1,0:T(8,128)(2,1)} fusion(bf16[8,1,2,72,1024]{4,3,2,1,0:T(8,128)(2,1)} %bitcast.19, bf16[8,1,2,72,1024]{4,3,2,1,0:T(8,128)(2,1)S(1)} %get-tuple-element.118), kind=kLoop, calls=%fused_computation | loop fusion | flops 2359296 | bytes 9437184 | tf_op jit(solution)/shard_map/stack | solution.py:431
  123.4 16.4 %forward.1 = (bf16[2048,512]{1,0:T(8,128)(2,1)}, bf16[2048,512]{1,0:T(8,128)(2,1)}, bf16[512,2048]{1,0:T(8,128)(2,1)}, f32[512,2048]{1,0:T(8,128)}) custom-call(s32[8]{0:T(128)} %copy-done.18, s32[8]{0:T(128)} %fusion.17.window_ref, s32[4]{0:T(128)} %copy-done.17, s32[1]{0:T(128)} %bitcast.13.core_ref, bf16[8,288,1024]{2,1,0:T(8,128)(2,1)} %bitcast.48, ...), custom_call_target="tpu_custom_call" | custom-call | flops 4563402752 | bytes 20971520 | tf_op jit(solution)/shard_map/forward/pallas_call | solution.py:160
  140.4 2.2 collective-permute-start.18
  142.6 4.6 %hidden_products.5 = (f32[512,512]{1,0:T(8,128)}, bf16[512,512]{1,0:T(8,128)(2,1)}) custom-call(s32[1]{0:T(128)} %bitcast.place_ref, bf16[256,2048]{1,0:T(8,128)(2,1)} %own_ref.7, bf16[256,2048]{1,0:T(8,128)(2,1)} %copy-done.1, bf16[256,1024]{1,0:T(8,128)(2,1)} %collective-permute-done.3.refs_0_.refs_6_, ...), custom_call_target="tpu_custom_call" | custom-call | flops 1073741824 | bytes 2097152 | tf_op jit(solution)/shard_map/hidden_products/pallas_call | solution.py:93
  147.2 2.7 %collective-permute-start.20 = (bf16[512,512]{1,0:T(8,128)(2,1)}, bf16[512,512]{1,0:T(8,128)(2,1)S(1)}, u32[]{:S(2)}, u32[]{:S(2)}) collective-permute-start(bf16[512,512]{1,0:T(8,128)(2,1)} %get-tuple-element.92), channel_id=1, source_target_pairs={{0,1},{1,0},{2,3},{3,2},{4,5},{5,4},{6,7},{7,6},{8,9},{9,8},{10,11... | collective-permute-start | bytes 1572872 | tf_op jit(solution)/shard_map/ppermute | solution.py:29
  150.0 2.7 %collective-permute-done.17.refs_2_.refs_5_ = bf16[256,1024]{1,0:T(8,128)(2,1)S(1)} collective-permute-done((bf16[256,1024]{1,0:T(8,128)(2,1)}, bf16[256,1024]{1,0:T(8,128)(2,1)S(1)}, u32[]{:S(2)}, u32[]{:S(2)}) %collective-permute-start.17) | collective-permute-done | bytes 524320 | tf_op jit(solution)/shard_map/ppermute | solution.py:39
  153.7 4.7 %hidden_products.6 = (f32[512,512]{1,0:T(8,128)}, bf16[512,512]{1,0:T(8,128)(2,1)}) custom-call(s32[1]{0:T(128)} %bitcast.place_ref, bf16[256,2048]{1,0:T(8,128)(2,1)} %own_ref.7, bf16[256,2048]{1,0:T(8,128)(2,1)} %copy-done.1, bf16[256,1024]{1,0:T(8,128)(2,1)} %collective-permute-done.10.refs_0_.refs_5_, ...), custom_call_target="tpu_custom_call" | custom-call | flops 1073741824 | bytes 2097152 | tf_op jit(solution)/shard_map/hidden_products/pallas_call | solution.py:93
  158.4 5.6 %collective-permute-start.21 = (bf16[512,512]{1,0:T(8,128)(2,1)}, bf16[512,512]{1,0:T(8,128)(2,1)S(1)}, u32[]{:S(2)}, u32[]{:S(2)}) collective-permute-start(bf16[512,512]{1,0:T(8,128)(2,1)} %get-tuple-element.86), channel_id=1, source_target_pairs={{0,1},{1,0},{2,3},{3,2},{4,5},{5,4},{6,7},{7,6},{8,9},{9,8},{10,11... | collective-permute-start | bytes 1572872 | tf_op jit(solution)/shard_map/ppermute | solution.py:29
  164.7 5.9 %summed_product.2 = bf16[512,1024]{1,0:T(8,128)(2,1)} custom-call(bf16[512,2048]{1,0:T(8,128)(2,1)} %get-tuple-element.93.left_ref, bf16[256,1024]{1,0:T(8,128)(2,1)} %get-tuple-element.123.refs_1_.refs_0_, bf16[256,1024]{1,0:T(8,128)(2,1)} %collective-permute-done.2.refs_2_.refs_1_, bf16[256,1024]{1,0:T(8,128)(2,1)} %collective-permute-done.4.refs_1_.refs_2_, ...), custom_call_target="tpu_custom_call" | custom-call | flops 2147483648 | bytes 10485760 | tf_op jit(solution)/shard_map/summed_product/pallas_call | solution.py:60
  170.7 6.7 %all-to-all-start.1 = ((bf16[16,32,1024]{2,1,0:T(8,128)(2,1)}), bf16[16,32,1024]{2,1,0:T(8,128)(2,1)S(1)}, u32[]{:S(2)}, u32[]{:S(2)}) async-start(bf16[16,32,1024]{2,1,0:T(8,128)(2,1)} %bitcast.56), calls=%async_computation.1 | async-start | bytes 2097152 | tf_op jit(solution)/shard_map/all_to_all | solution.py:459
  179.4 8.3 %input_products.1 = (f32[512,512]{1,0:T(8,128)}, f32[512,512]{1,0:T(8,128)}, f32[8,512]{1,0:T(8,128)}) custom-call(f32[512,768]{1,0:T(8,128)} %get-tuple-element.88.refs_0_, f32[512,512]{1,0:T(8,128)} %get-tuple-element.89.refs_1_, f32[512,512]{1,0:T(8,128)} %get-tuple-element.90.refs_2_, bf16[512,768]{1,0:T(8,128)(2,1)} %copy-done.5, ...), custom_call_target="tpu_custom_call" | custom-call | flops 1879048192 | bytes 8388608 | tf_op jit(solution)/shard_map/input_products/pallas_call | solution.py:243
  188.7 3.5 %hidden_products.7 = (f32[512,256]{1,0:T(8,128)}, bf16[512,256]{1,0:T(8,128)(2,1)}) custom-call(s32[1]{0:T(128)} %bitcast.place_ref, bf16[256,2048]{1,0:T(8,128)(2,1)} %own_ref.7, bf16[256,2048]{1,0:T(8,128)(2,1)} %copy-done.1, bf16[256,1024]{1,0:T(8,128)(2,1)} %copy-done.10, bf16[256,1024]{1,0:T(8,128)(2,1)} %copy-done.9), custom_call_target="tpu_custom_call" | custom-call | flops 536870912 | bytes 1048576 | tf_op jit(solution)/shard_map/hidden_products/pallas_call | solution.py:93
  192.2 4.1 %collective-permute-start.22 = (bf16[512,256]{1,0:T(8,128)(2,1)}, bf16[512,256]{1,0:T(8,128)(2,1)S(1)}, u32[]{:S(2)}, u32[]{:S(2)}) collective-permute-start(bf16[512,256]{1,0:T(8,128)(2,1)} %get-tuple-element.105), channel_id=1, source_target_pairs={{0,1},{1,0},{2,3},{3,2},{4,5},{5,4},{6,7},{7,6},{8,9},{9,8},{10,11... | collective-permute-start | bytes 786440 | tf_op jit(solution)/shard_map/ppermute | solution.py:29
  196.3 1.4 collective-permute-done.22.other_ref
  198.4 4.1 %input_pieces.1 = bf16[16,96,256]{2,1,0:T(8,128)(2,1)} custom-call(f32[512,256]{1,0:T(8,128)} %get-tuple-element.104.part_ref, bf16[512,256]{1,0:T(8,128)(2,1)} %copy-done.13, f32[512,2048]{1,0:T(8,128)} %get-tuple-element.97.refs_6_.slope_ref, bf16[2048,512]{1,0:T(8,128)(2,1)} %get-tuple-element.98.refs_7_.in_ref, ...), custom_call_target="tpu_custom_call" | custom-call | flops 268435456 | bytes 1048576 | tf_op jit(solution)/shard_map/input_pieces/pallas_call | solution.py:315
  202.5 6.7 %all-to-all-start.2 = ((bf16[16,96,256]{2,1,0:T(8,128)(2,1)}), bf16[16,96,256]{2,1,0:T(8,128)(2,1)S(1)}, u32[]{:S(2)}, u32[]{:S(2)}) async-start(bf16[16,96,256]{2,1,0:T(8,128)(2,1)} %input_pieces.1), calls=%async_computation.2 | async-start | bytes 1572864 | tf_op jit(solution)/shard_map/all_to_all | solution.py:469
  209.3 6.0 %summed_product.3 = bf16[512,1024]{1,0:T(8,128)(2,1)} custom-call(bf16[512,2048]{1,0:T(8,128)(2,1)} %get-tuple-element.93.left_ref, bf16[256,1024]{1,0:T(8,128)(2,1)} %get-tuple-element.122.refs_4_.refs_0_, bf16[256,1024]{1,0:T(8,128)(2,1)} %copy-done.20, bf16[256,1024]{1,0:T(8,128)(2,1)} %collective-permute-done.13.refs_3_.refs_2_, ...), custom_call_target="tpu_custom_call" | custom-call | flops 2147483648 | bytes 10485760 | tf_op jit(solution)/shard_map/summed_product/pallas_call | solution.py:60
  215.3 6.2 %all-to-all-done.2 = bf16[16,96,256]{2,1,0:T(8,128)(2,1)S(1)} async-done(((bf16[16,96,256]{2,1,0:T(8,128)(2,1)}), bf16[16,96,256]{2,1,0:T(8,128)(2,1)S(1)}, u32[]{:S(2)}, u32[]{:S(2)}) %all-to-all-start.2) | async-done | bytes 786464 | tf_op jit(solution)/shard_map/all_to_all | solution.py:469
  222.8 1.9 collective-permute-done.23
  224.7 2.7 %collective-permute-start.24 = (f32[28,256]{1,0:T(8,128)S(1)}, f32[28,256]{1,0:T(8,128)S(1)}, u32[]{:S(2)}, u32[]{:S(2)}) collective-permute-start(f32[28,256]{1,0:T(8,128)S(1)} %fusion.18), channel_id=1, source_target_pairs={{0,64},{32,96},{64,0},{96,32},{128,192},{160,224},{192,128},{224,1... | collective-permute-start | bytes 86024 | tf_op jit(solution)/shard_map/ppermute | solution.py:489
  227.4 1.3 collective-permute-done.24
  228.7 4.7 %collective-permute-start.25 = (f32[28,256]{1,0:T(8,128)S(1)}, f32[28,256]{1,0:T(8,128)S(1)}, u32[]{:S(2)}, u32[]{:S(2)}) collective-permute-start(f32[28,256]{1,0:T(8,128)S(1)} %add.93), channel_id=1, source_target_pairs={{0,128},{32,160},{64,192},{96,224},{128,0},{160,32},{192,64},{224,... | collective-permute-start | bytes 86024 | tf_op jit(solution)/shard_map/ppermute | solution.py:489
  233.4 2.0 collective-permute-done.25
  235.4 5.3 %collective-permute-start.26 = (f32[28,256]{1,0:T(8,128)S(1)}, f32[28,256]{1,0:T(8,128)S(1)}, u32[]{:S(2)}, u32[]{:S(2)}) collective-permute-start(f32[28,256]{1,0:T(8,128)S(1)} %add.94), channel_id=1, source_target_pairs={{0,1},{1,0},{2,3},{3,2},{4,5},{5,4},{6,7},{7,6},{8,9},{9,8},{10,11... | collective-permute-start | bytes 86024 | tf_op jit(solution)/shard_map/ppermute | solution.py:29
  241.5 3.8 %all-to-all-start.3 = ((bf16[16,32,1024]{2,1,0:T(8,128)(2,1)}), bf16[16,32,1024]{2,1,0:T(8,128)(2,1)S(1)}, u32[]{:S(2)}, u32[]{:S(2)}) async-start(bf16[16,32,1024]{2,1,0:T(8,128)(2,1)} %bitcast.26), calls=%async_computation.3 | async-start | bytes 2097152 | tf_op jit(solution)/shard_map/all_to_all | solution.py:471
  248.3 13.2 %all-to-all-done.3 = bf16[16,32,1024]{2,1,0:T(8,128)(2,1)S(1)} async-done(((bf16[16,32,1024]{2,1,0:T(8,128)(2,1)}), bf16[16,32,1024]{2,1,0:T(8,128)(2,1)S(1)}, u32[]{:S(2)}, u32[]{:S(2)}) %all-to-all-start.3) | async-done | bytes 1048608 | tf_op jit(solution)/shard_map/all_to_all | solution.py:471
  (148 shorter events, 34.0 us)
Async XLA Ops:
  0.6 13.2 %copy-start.4 = (bf16[1,256,2048]{2,1,0:T(8,128)(2,1)S(1)}, bf16[1,256,2048]{2,1,0:T(8,128)(2,1)}, u32[]{:S(2)}) copy-start(bf16[1,256,2048]{2,1,0:T(8,128)(2,1)} %param.15) | copy-start | bytes 3145732
  1.8 16.7 %collective-permute-start.7 = (bf16[512,256]{0,1:T(8,128)(2,1)S(1)}, bf16[512,256]{0,1:T(8,128)(2,1)S(1)}, u32[]{:S(2)}, u32[]{:S(2)}) collective-permute-start(bf16[512,256]{0,1:T(8,128)(2,1)S(1)} %copy.50), channel_id=1, source_target_pairs={{0,1},{1,0},{2,3},{3,2},{4,5},{5,4},{6,7},{7,6},{8,9},{9,8},{10,11... | collective-permute-start | bytes 786440 | tf_op jit(solution)/shard_map/ppermute | solution.py:29
  7.2 9.1 %copy-start = (bf16[256,2048]{1,0:T(8,128)(2,1)S(1)}, bf16[256,2048]{1,0:T(8,128)(2,1)}, u32[]{:S(2)}) copy-start(bf16[256,2048]{1,0:T(8,128)(2,1)} %own_ref.7) | copy-start | bytes 3145732
  7.2 10.4 %copy-start.14 = (s32[1,2304]{1,0:T(1,128)S(1)}, s32[1,2304]{1,0:T(1,128)}, u32[]{:S(2)}) copy-start(s32[1,2304]{1,0:T(1,128)} %param.17) | copy-start | bytes 27652
  7.2 10.4 %copy-start.15 = (s32[1,2]{1,0:T(1,128)S(1)}, s32[1,2]{1,0:T(1,128)}, u32[]{:S(2)}) copy-start(s32[1,2]{1,0:T(1,128)} %param.16) | copy-start | bytes 28
  7.2 10.6 %copy-start.16 = (f32[256]{0:T(256)S(1)}, f32[256]{0:T(256)}, u32[]{:S(2)}) copy-start(f32[256]{0:T(256)} %param.13) | copy-start | bytes 3076
  7.2 55.0 %all-to-all-start = ((bf16[8,72,1024]{2,1,0:T(8,128)(2,1)}), bf16[8,72,1024]{2,1,0:T(8,128)(2,1)}, u32[]{:S(2)}, u32[]{:S(2)}) async-start(bf16[8,72,1024]{2,1,0:T(8,128)(2,1)} %broadcast_in_dim.60), calls=%async_computation | async-start | bytes 2359296 | tf_op jit(solution)/shard_map/all_to_all | solution.py:366
  14.9 50.2 %collective-permute-start.1 = (bf16[256,1024]{1,0:T(8,128)(2,1)}, bf16[256,1024]{1,0:T(8,128)(2,1)}, u32[]{:S(2)}, u32[]{:S(2)}) collective-permute-start(bf16[256,1024]{1,0:T(8,128)(2,1)} %get-tuple-element.123.refs_1_.refs_0_), channel_id=1, source_target_pairs={{0,32},{32,64},{64,96},{96,128},{128,160},{160,192},{192,224},{224... | collective-permute-start | bytes 1572872 | tf_op jit(solution)/shard_map/ppermute | solution.py:39
  16.3 70.2 %collective-permute-start = (bf16[256,2048]{1,0:T(8,128)(2,1)S(1)}, bf16[256,2048]{1,0:T(8,128)(2,1)S(1)}, u32[]{:S(2)}, u32[]{:S(2)}) collective-permute-start(bf16[256,2048]{1,0:T(8,128)(2,1)S(1)} %copy-done), channel_id=1, source_target_pairs={{0,16},{16,0},{1,17},{17,1},{2,18},{18,2},{3,19},{19,3},{4,20},{20... | collective-permute-start | bytes 3145736 | tf_op jit(solution)/shard_map/ppermute | solution.py:29
  18.1 2.5 copy-start.17
  18.2 2.2 copy-start.18
  20.0 31.6 %collective-permute-start.8 = (bf16[1032,256]{1,0:T(8,128)(2,1)}, bf16[1032,256]{1,0:T(8,128)(2,1)S(1)}, u32[]{:S(2)}, u32[]{:S(2)}) collective-permute-start(bf16[1032,256]{1,0:T(8,128)(2,1)} %copy.55), channel_id=1, source_target_pairs={{0,16},{16,0},{1,17},{17,1},{2,18},{18,2},{3,19},{19,3},{4,20},{20... | collective-permute-start | bytes 1585160 | tf_op jit(solution)/shard_map/ppermute | solution.py:29
  53.9 0.8 copy-start.2
  55.8 6.3 %copy-start.3 = (bf16[1032,256]{0,1:T(8,128)(2,1)S(1)}, bf16[1032,256]{0,1:T(8,128)(2,1)}, u32[]{:S(2)}) copy-start(bf16[1032,256]{0,1:T(8,128)(2,1)} %copy-done.2) | copy-start | bytes 1585156
  62.2 32.0 %collective-permute-start.9 = (bf16[8,72,1024]{2,1,0:T(8,128)(2,1)}, bf16[8,72,1024]{2,1,0:T(8,128)(2,1)S(1)}, u32[]{:S(2)}, u32[]{:S(2)}) collective-permute-start(bf16[8,72,1024]{2,1,0:T(8,128)(2,1)} %all-to-all-done), channel_id=1, source_target_pairs={{0,16},{16,0},{1,17},{17,1},{2,18},{18,2},{3,19},{19,3},{4,20},{20... | collective-permute-start | bytes 3538952 | tf_op jit(solution)/shard_map/ppermute | solution.py:29
  63.5 11.9 %collective-permute-start.2 = (bf16[256,1024]{1,0:T(8,128)(2,1)}, bf16[256,1024]{1,0:T(8,128)(2,1)}, u32[]{:S(2)}, u32[]{:S(2)}) collective-permute-start(bf16[256,1024]{1,0:T(8,128)(2,1)} %get-tuple-element.123.refs_1_.refs_0_), channel_id=1, source_target_pairs={{0,224},{32,0},{64,32},{96,64},{128,96},{160,128},{192,160},{224,1... | collective-permute-start | bytes 1572872 | tf_op jit(solution)/shard_map/ppermute | solution.py:39
  65.0 13.0 %collective-permute-start.5 = (bf16[256,1024]{1,0:T(8,128)(2,1)}, bf16[256,1024]{1,0:T(8,128)(2,1)S(1)}, u32[]{:S(2)}, u32[]{:S(2)}) collective-permute-start(bf16[256,1024]{1,0:T(8,128)(2,1)} %get-tuple-element.122.refs_4_.refs_0_), channel_id=1, source_target_pairs={{0,32},{32,64},{64,96},{96,128},{128,160},{160,192},{192,224},{224... | collective-permute-start | bytes 1572872 | tf_op jit(solution)/shard_map/ppermute | solution.py:39
  65.0 21.5 %collective-permute-start.6 = (bf16[256,1024]{1,0:T(8,128)(2,1)}, bf16[256,1024]{1,0:T(8,128)(2,1)S(1)}, u32[]{:S(2)}, u32[]{:S(2)}) collective-permute-start(bf16[256,1024]{1,0:T(8,128)(2,1)} %get-tuple-element.122.refs_4_.refs_0_), channel_id=1, source_target_pairs={{0,224},{32,0},{64,32},{96,64},{128,96},{160,128},{192,160},{224,1... | collective-permute-start | bytes 1572872 | tf_op jit(solution)/shard_map/ppermute | solution.py:39
  78.0 8.5 %copy-start.19 = (bf16[256,1024]{1,0:T(8,128)(2,1)}, bf16[256,1024]{1,0:T(8,128)(2,1)S(1)}, u32[]{:S(2)}) copy-start(bf16[256,1024]{1,0:T(8,128)(2,1)S(1)} %collective-permute-done.5.refs_3_.refs_7_) | copy-start | bytes 1572868
  86.6 0.8 copy-start.20
  87.4 1.0 copy-start.1
  97.2 21.0 %collective-permute-start.14 = (bf16[8,2,72,1024]{3,2,1,0:T(8,128)(2,1)}, bf16[8,2,72,1024]{3,2,1,0:T(8,128)(2,1)}, u32[]{:S(2)}, u32[]{:S(2)}) collective-permute-start(bf16[8,2,72,1024]{3,2,1,0:T(8,128)(2,1)} %get-tuple-element.119), channel_id=1, source_target_pairs={{0,1},{1,0},{2,3},{3,2},{4,5},{5,4},{6,7},{7,6},{8,9},{9,8},{10,11... | collective-permute-start | bytes 7077896 | tf_op jit(solution)/shard_map/ppermute | solution.py:29
  99.9 15.1 %collective-permute-start.3 = (bf16[256,1024]{1,0:T(8,128)(2,1)}, bf16[256,1024]{1,0:T(8,128)(2,1)}, u32[]{:S(2)}, u32[]{:S(2)}) collective-permute-start(bf16[256,1024]{1,0:T(8,128)(2,1)} %collective-permute-done.1.refs_0_.refs_7_), channel_id=1, source_target_pairs={{0,32},{32,64},{64,96},{96,128},{128,160},{160,192},{192,224},{224... | collective-permute-start | bytes 1572872 | tf_op jit(solution)/shard_map/ppermute | solution.py:39
  101.1 15.3 %collective-permute-start.4 = (bf16[256,1024]{1,0:T(8,128)(2,1)}, bf16[256,1024]{1,0:T(8,128)(2,1)}, u32[]{:S(2)}, u32[]{:S(2)}) collective-permute-start(bf16[256,1024]{1,0:T(8,128)(2,1)} %collective-permute-done.2.refs_2_.refs_1_), channel_id=1, source_target_pairs={{0,224},{32,0},{64,32},{96,64},{128,96},{160,128},{192,160},{224,1... | collective-permute-start | bytes 1572872 | tf_op jit(solution)/shard_map/ppermute | solution.py:39
  106.4 33.4 %collective-permute-start.15 = (bf16[512,768]{1,0:T(8,128)(2,1)}, bf16[512,768]{1,0:T(8,128)(2,1)S(1)}, u32[]{:S(2)}, u32[]{:S(2)}) collective-permute-start(bf16[512,768]{1,0:T(8,128)(2,1)} %get-tuple-element.68), channel_id=1, source_target_pairs={{0,1},{1,0},{2,3},{3,2},{4,5},{5,4},{6,7},{7,6},{8,9},{9,8},{10,11... | collective-permute-start | bytes 2359304 | tf_op jit(solution)/shard_map/ppermute | solution.py:29
  107.6 32.2 %collective-permute-start.12 = (bf16[256,1024]{1,0:T(8,128)(2,1)}, bf16[256,1024]{1,0:T(8,128)(2,1)}, u32[]{:S(2)}, u32[]{:S(2)}) collective-permute-start(bf16[256,1024]{1,0:T(8,128)(2,1)} %copy-done.19), channel_id=1, source_target_pairs={{0,32},{32,64},{64,96},{96,128},{128,160},{160,192},{192,224},{224... | collective-permute-start | bytes 1572872 | tf_op jit(solution)/shard_map/ppermute | solution.py:39
  115.0 24.8 %collective-permute-start.13 = (bf16[256,1024]{1,0:T(8,128)(2,1)}, bf16[256,1024]{1,0:T(8,128)(2,1)}, u32[]{:S(2)}, u32[]{:S(2)}) collective-permute-start(bf16[256,1024]{1,0:T(8,128)(2,1)} %copy-done.20), channel_id=1, source_target_pairs={{0,224},{32,0},{64,32},{96,64},{128,96},{160,128},{192,160},{224,1... | collective-permute-start | bytes 1572872 | tf_op jit(solution)/shard_map/ppermute | solution.py:39
  116.5 26.2 %collective-permute-start.10 = (bf16[256,1024]{1,0:T(8,128)(2,1)}, bf16[256,1024]{1,0:T(8,128)(2,1)}, u32[]{:S(2)}, u32[]{:S(2)}) collective-permute-start(bf16[256,1024]{1,0:T(8,128)(2,1)} %collective-permute-done.3.refs_0_.refs_6_), channel_id=1, source_target_pairs={{0,32},{32,64},{64,96},{96,128},{128,160},{160,192},{192,224},{224... | collective-permute-start | bytes 1572872 | tf_op jit(solution)/shard_map/ppermute | solution.py:39
  118.2 24.4 %collective-permute-start.11 = (bf16[256,1024]{1,0:T(8,128)(2,1)}, bf16[256,1024]{1,0:T(8,128)(2,1)}, u32[]{:S(2)}, u32[]{:S(2)}) collective-permute-start(bf16[256,1024]{1,0:T(8,128)(2,1)} %collective-permute-done.4.refs_1_.refs_2_), channel_id=1, source_target_pairs={{0,224},{32,0},{64,32},{96,64},{128,96},{160,128},{192,160},{224,1... | collective-permute-start | bytes 1572872 | tf_op jit(solution)/shard_map/ppermute | solution.py:39
  139.8 7.4 %copy-start.5 = (bf16[512,768]{1,0:T(8,128)(2,1)}, bf16[512,768]{1,0:T(8,128)(2,1)S(1)}, u32[]{:S(2)}) copy-start(bf16[512,768]{1,0:T(8,128)(2,1)S(1)} %collective-permute-done.15.refs_3_) | copy-start | bytes 2359300
  139.8 12.8 %collective-permute-start.17 = (bf16[256,1024]{1,0:T(8,128)(2,1)}, bf16[256,1024]{1,0:T(8,128)(2,1)S(1)}, u32[]{:S(2)}, u32[]{:S(2)}) collective-permute-start(bf16[256,1024]{1,0:T(8,128)(2,1)} %collective-permute-done.12.refs_2_.refs_6_), channel_id=1, source_target_pairs={{0,32},{32,64},{64,96},{96,128},{128,160},{160,192},{192,224},{224... | collective-permute-start | bytes 1572872 | tf_op jit(solution)/shard_map/ppermute | solution.py:39
  140.4 12.3 %collective-permute-start.18 = (bf16[256,1024]{1,0:T(8,128)(2,1)}, bf16[256,1024]{1,0:T(8,128)(2,1)S(1)}, u32[]{:S(2)}, u32[]{:S(2)}) collective-permute-start(bf16[256,1024]{1,0:T(8,128)(2,1)} %collective-permute-done.13.refs_3_.refs_2_), channel_id=1, source_target_pairs={{0,224},{32,0},{64,32},{96,64},{128,96},{160,128},{192,160},{224,1... | collective-permute-start | bytes 1572872 | tf_op jit(solution)/shard_map/ppermute | solution.py:39
  142.6 21.3 %collective-permute-start.16 = (bf16[256,1024]{1,0:T(8,128)(2,1)}, bf16[256,1024]{1,0:T(8,128)(2,1)S(1)}, u32[]{:S(2)}, u32[]{:S(2)}) collective-permute-start(bf16[256,1024]{1,0:T(8,128)(2,1)} %collective-permute-done.10.refs_0_.refs_5_), channel_id=1, source_target_pairs={{0,32},{32,64},{64,96},{96,128},{128,160},{160,192},{192,224},{224... | collective-permute-start | bytes 1572872 | tf_op jit(solution)/shard_map/ppermute | solution.py:39
  147.2 30.5 %collective-permute-start.20 = (bf16[512,512]{1,0:T(8,128)(2,1)}, bf16[512,512]{1,0:T(8,128)(2,1)S(1)}, u32[]{:S(2)}, u32[]{:S(2)}) collective-permute-start(bf16[512,512]{1,0:T(8,128)(2,1)} %get-tuple-element.92), channel_id=1, source_target_pairs={{0,1},{1,0},{2,3},{3,2},{4,5},{5,4},{6,7},{7,6},{8,9},{9,8},{10,11... | collective-permute-start | bytes 1572872 | tf_op jit(solution)/shard_map/ppermute | solution.py:29
  152.7 0.8 copy-start.6
  152.7 1.0 copy-start.7
  158.4 19.4 %collective-permute-start.21 = (bf16[512,512]{1,0:T(8,128)(2,1)}, bf16[512,512]{1,0:T(8,128)(2,1)S(1)}, u32[]{:S(2)}, u32[]{:S(2)}) collective-permute-start(bf16[512,512]{1,0:T(8,128)(2,1)} %get-tuple-element.86), channel_id=1, source_target_pairs={{0,1},{1,0},{2,3},{3,2},{4,5},{5,4},{6,7},{7,6},{8,9},{9,8},{10,11... | collective-permute-start | bytes 1572872 | tf_op jit(solution)/shard_map/ppermute | solution.py:29
  170.7 6.7 %copy-start.8 = (bf16[256,1024]{1,0:T(8,128)(2,1)S(1)}, bf16[256,1024]{1,0:T(8,128)(2,1)}, u32[]{:S(2)}) copy-start(bf16[256,1024]{1,0:T(8,128)(2,1)} %copy-done.7) | copy-start | bytes 1572868
  170.7 31.8 %all-to-all-start.1 = ((bf16[16,32,1024]{2,1,0:T(8,128)(2,1)}), bf16[16,32,1024]{2,1,0:T(8,128)(2,1)S(1)}, u32[]{:S(2)}, u32[]{:S(2)}) async-start(bf16[16,32,1024]{2,1,0:T(8,128)(2,1)} %bitcast.56), calls=%async_computation.1 | async-start | bytes 2097152 | tf_op jit(solution)/shard_map/all_to_all | solution.py:459
  177.4 10.6 %collective-permute-start.19 = (bf16[256,1024]{1,0:T(8,128)(2,1)S(1)}, bf16[256,1024]{1,0:T(8,128)(2,1)S(1)}, u32[]{:S(2)}, u32[]{:S(2)}) collective-permute-start(bf16[256,1024]{1,0:T(8,128)(2,1)S(1)} %copy-done.8), channel_id=1, source_target_pairs={{0,224},{32,0},{64,32},{96,64},{128,96},{160,128},{192,160},{224,1... | collective-permute-start | bytes 1572872 | tf_op jit(solution)/shard_map/ppermute | solution.py:39
  177.8 0.8 copy-start.11
  192.2 5.4 %collective-permute-start.22 = (bf16[512,256]{1,0:T(8,128)(2,1)}, bf16[512,256]{1,0:T(8,128)(2,1)S(1)}, u32[]{:S(2)}, u32[]{:S(2)}) collective-permute-start(bf16[512,256]{1,0:T(8,128)(2,1)} %get-tuple-element.105), channel_id=1, source_target_pairs={{0,1},{1,0},{2,3},{3,2},{4,5},{5,4},{6,7},{7,6},{8,9},{9,8},{10,11... | collective-permute-start | bytes 786440 | tf_op jit(solution)/shard_map/ppermute | solution.py:29
  202.5 19.0 %all-to-all-start.2 = ((bf16[16,96,256]{2,1,0:T(8,128)(2,1)}), bf16[16,96,256]{2,1,0:T(8,128)(2,1)S(1)}, u32[]{:S(2)}, u32[]{:S(2)}) async-start(bf16[16,96,256]{2,1,0:T(8,128)(2,1)} %input_pieces.1), calls=%async_computation.2 | async-start | bytes 1572864 | tf_op jit(solution)/shard_map/all_to_all | solution.py:469
  221.8 2.9 %collective-permute-start.23 = (f32[28,256]{1,0:T(8,128)S(1)}, f32[28,256]{1,0:T(8,128)S(1)}, u32[]{:S(2)}, u32[]{:S(2)}) collective-permute-start(f32[28,256]{1,0:T(8,128)S(1)} %pad_maximum_fusion.4), channel_id=1, source_target_pairs={{0,32},{32,0},{64,96},{96,64},{128,160},{160,128},{192,224},{224,1... | collective-permute-start | bytes 86024 | tf_op jit(solution)/shard_map/ppermute | solution.py:489
  224.7 4.0 %collective-permute-start.24 = (f32[28,256]{1,0:T(8,128)S(1)}, f32[28,256]{1,0:T(8,128)S(1)}, u32[]{:S(2)}, u32[]{:S(2)}) collective-permute-start(f32[28,256]{1,0:T(8,128)S(1)} %fusion.18), channel_id=1, source_target_pairs={{0,64},{32,96},{64,0},{96,32},{128,192},{160,224},{192,128},{224,1... | collective-permute-start | bytes 86024 | tf_op jit(solution)/shard_map/ppermute | solution.py:489
  228.7 6.7 %collective-permute-start.25 = (f32[28,256]{1,0:T(8,128)S(1)}, f32[28,256]{1,0:T(8,128)S(1)}, u32[]{:S(2)}, u32[]{:S(2)}) collective-permute-start(f32[28,256]{1,0:T(8,128)S(1)} %add.93), channel_id=1, source_target_pairs={{0,128},{32,160},{64,192},{96,224},{128,0},{160,32},{192,64},{224,... | collective-permute-start | bytes 86024 | tf_op jit(solution)/shard_map/ppermute | solution.py:489
  235.4 9.9 %collective-permute-start.26 = (f32[28,256]{1,0:T(8,128)S(1)}, f32[28,256]{1,0:T(8,128)S(1)}, u32[]{:S(2)}, u32[]{:S(2)}) collective-permute-start(f32[28,256]{1,0:T(8,128)S(1)} %add.94), channel_id=1, source_target_pairs={{0,1},{1,0},{2,3},{3,2},{4,5},{5,4},{6,7},{7,6},{8,9},{9,8},{10,11... | collective-permute-start | bytes 86024 | tf_op jit(solution)/shard_map/ppermute | solution.py:29
  241.5 20.0 %all-to-all-start.3 = ((bf16[16,32,1024]{2,1,0:T(8,128)(2,1)}), bf16[16,32,1024]{2,1,0:T(8,128)(2,1)S(1)}, u32[]{:S(2)}, u32[]{:S(2)}) async-start(bf16[16,32,1024]{2,1,0:T(8,128)(2,1)} %bitcast.26), calls=%async_computation.3 | async-start | bytes 2097152 | tf_op jit(solution)/shard_map/all_to_all | solution.py:471
  (4 other events, 3.1 us)
where the time goes:
time: 263 us; the launch traced here: 262 us
  waiting for transfers between devices  82.5 us (31%)
  starting transfers between devices  74.9 us (28%)
  Pallas kernels  59.5 us (23%)
  local copies, waits for them, and re-layouts  29.3 us (11%)
  other arithmetic  13.7 us (5%)
    ppermute x10, waiting for transfers between devices, swap(): return lax.ppermute(array, axis, [(0, 1), (1, 0)])  29.6 us
    ppermute x14, waiting for transfers between devices, along_z(): lax.ppermute(array, 'z', [(i, (i + shift) % count) for i in range(count)])  28.2 us
    ppermute x10, starting transfers between devices, swap(): return lax.ppermute(array, axis, [(0, 1), (1, 0)])  27.1 us
    pallas_call x4, Pallas kernels, hidden_products(): pl.pallas_call(kernel, grid_spec=pltpu.PrefetchScalarGridSpec(num_scalar_...  18.7 us
    pallas_call x1, Pallas kernels, forward(): pl.pallas_call(kernel, grid_spec=pltpu.PrefetchScalarGridSpec(num_scalar_...  16.4 us
    ppermute x14, starting transfers between devices, along_z(): lax.ppermute(array, 'z', [(i, (i + shift) % count) for i in range(count)])  15.8 us
    all_to_all x1, waiting for transfers between devices, one_step(): high_moved = lax.all_to_all(high_product, PLANE, 0, 0, tiled=True)  13.2 us
    pallas_call x2, Pallas kernels, summed_product(): pl.pallas_call(kernel, grid=(width // tile,), in_specs=[whole(left.shape)...  11.9 us
  transfers between devices with their start and end apart: 31, of which 13 were waited for; matrix products, arithmetic and copies ran while one was open for 12% of the time, Pallas kernels for 23%

commit v1 on v0

--- a/solution.py
+++ b/solution.py
@@ -406,11 +406,12 @@
         parts = vector.reshape(img_count, 2, piece)
         return lax.dynamic_index_in_dim(parts, core, 1, False).reshape(1, -1)
 
-    seen, w_turned, w_own, b_column, out_part, held_pos = gate(
-        seen, w_turned, w_own, b_column, out_part, held_pos
-    )
     seen_other = swap(seen, "xl")
-    low[7], low[1] = gate(low[7], low[1])
+    gains = (ln_gain[None, :], own_part(ln_gain))
+    biases = (ln_bias[None, :], own_part(ln_bias))
+    low[7], low[1], w_turned, w_own, b_column, out_part, held_pos, window_starts, gains, biases = gate(
+        low[7], low[1], w_turned, w_own, b_column, out_part, held_pos, window_starts, gains, biases
+    )
     low[6], low[2] = along_z(low[7], 1), along_z(low[1], -1)
     high[7], high[1] = gate(high[7], high[1])
     high[6], high[2] = along_z(high[7], 1), along_z(high[1], -1)
@@ -419,15 +420,17 @@
     def products(blocks):
         return hidden_products(weights, place, [low[i] for i in blocks], [high[i] for i in blocks])
 
-    groups = [(7, 0, 1), (6, 2), (5, 3)]
-    parts, others = [None] * 3, [None] * 3
-    parts[0], rounded = products(groups[0])
-    parts[0], rounded, seen_other = gate(parts[0], rounded, seen_other)
+    groups = [(7, 1), (6, 2), (5, 3), (0,)]
+    parts, others = [None] * 4, [None] * 4
+    parts[3], rounded_own = products(groups[3])
+    parts[3], rounded_own, seen_other = gate(parts[3], rounded_own, seen_other)
     seen = jnp.stack([seen, seen_other], axis=1)
     seen_other = swap(seen, "c")
+    others[3] = swap(rounded_own, "c")
+    low[6], low[2] = gate(low[6], low[2])
+    low[5], low[3] = along_z(low[6], 1), along_z(low[2], -1)
+    parts[0], rounded = products(groups[0])
     others[0] = swap(rounded, "c")
-    low[6], low[2], rounded = gate(low[6], low[2], rounded)
-    low[5], low[3] = along_z(low[6], 1), along_z(low[2], -1)
     seen = jnp.stack([seen, seen_other], axis=1).reshape(z_count, of_z, feats)
     normed_in, normed, hidden, slope = forward(
         seen,
@@ -437,15 +440,17 @@
         image_starts,
         w_turned,
         b_column,
-        (ln_gain[None, :], own_part(ln_gain)),
-        (ln_bias[None, :], own_part(ln_bias)),
+        gains,
+        biases,
         core.reshape(1),
         rows,
         piece,
     )
-    high[6], high[2], hidden, others[0] = gate(high[6], high[2], hidden, others[0])
+    high[6], high[2] = gate(high[6], high[2])
     high[5], high[3] = along_z(high[6], 1), along_z(high[2], -1)
-    low[5], low[3], hidden = gate(low[5], low[3], hidden)
+    low[5], low[3], hidden, others[0], others[3] = gate(
+        low[5], low[3], hidden, others[0], others[3]
+    )
     low[4] = along_z(low[5], 1)
     parts[1], rounded = products(groups[1])
     others[1] = swap(rounded, "c")

time: 263 us -> 265 us (level)
  starting transfers between devices: 74.9 us -> 57.1 us
  waiting for transfers between devices: 82.5 us -> 94.7 us
    all_to_all x1, waiting for transfers between devices: 0.01 us -> 23.8 us  [one_step(): seen = lax.all_to_all(copies, 'z', 0, 0, tiled=True)]
    ppermute x14, waiting for transfers between devices: 28.2 us -> 16 us  [along_z(): lax.ppermute(array, 'z', [(i, (i + shift) % count) for i in range(count)])]
    ppermute x10 -> x11, starting transfers between devices: 27.1 us -> 18.5 us  [swap(): return lax.ppermute(array, axis, [(0, 1), (1, 0)])]
    ppermute x3, starting transfers between devices: 8.33 us -> 2.35 us  [one_step(): moved = lax.ppermute(vectors, 'z', [(i, i ^ shift) for i in range(z_count)])]
    ppermute x3, waiting for transfers between devices: 5.19 us -> 11 us  [one_step(): moved = lax.ppermute(vectors, 'z', [(i, i ^ shift) for i in range(z_count)])]
    ppermute x14, starting transfers between devices: 15.8 us -> 10.3 us  [along_z(): lax.ppermute(array, 'z', [(i, (i + shift) % count) for i in range(count)])]
    ppermute x10 -> x11, waiting for transfers between devices: 29.6 us -> 24.5 us  [swap(): return lax.ppermute(array, axis, [(0, 1), (1, 0)])]
    pallas_call x4 -> x5, Pallas kernels: 18.7 us -> 21.1 us  [hidden_products(): pl.pallas_call(kernel, grid_spec=pltpu.PrefetchScalarGridSpec(num_scalar_...]
  transfers between devices with their start and end apart: 31 -> 32, of which waited for: 13 -> 13; matrix products, arithmetic and copies ran while one was open for 12% -> 15% of each run, Pallas kernels for 23% -> 23%
where the time goes in v1:
time: 265 us; the launch traced here: 264 us
  waiting for transfers between devices  94.7 us (36%)
  Pallas kernels  61.9 us (23%)
  starting transfers between devices  57.1 us (22%)
  local copies, waits for them, and re-layouts  31.4 us (12%)
  other arithmetic  15.5 us (6%)
    ppermute x11, waiting for transfers between devices, swap(): return lax.ppermute(array, axis, [(0, 1), (1, 0)])  24.5 us
    all_to_all x1, waiting for transfers between devices, one_step(): seen = lax.all_to_all(copies, 'z', 0, 0, tiled=True)  23.8 us
    pallas_call x5, Pallas kernels, hidden_products(): pl.pallas_call(kernel, grid_spec=pltpu.PrefetchScalarGridSpec(num_scalar_...  21.1 us
    ppermute x11, starting transfers between devices, swap(): return lax.ppermute(array, axis, [(0, 1), (1, 0)])  18.5 us
    pallas_call x1, Pallas kernels, forward(): pl.pallas_call(kernel, grid_spec=pltpu.PrefetchScalarGridSpec(num_scalar_...  16.4 us
    ppermute x14, waiting for transfers between devices, along_z(): lax.ppermute(array, 'z', [(i, (i + shift) % count) for i in range(count)])  16 us
    all_to_all x1, waiting for transfers between devices, one_step(): high_moved = lax.all_to_all(high_product, PLANE, 0, 0, tiled=True)  13.2 us
    pallas_call x2, Pallas kernels, summed_product(): pl.pallas_call(kernel, grid=(width // tile,), in_specs=[whole(left.shape)...  11.9 us
  transfers between devices with their start and end apart: 32, of which 13 were waited for; matrix products, arithmetic and copies ran while one was open for 15% of the time, Pallas kernels for 23%

profile of v1, /device:TPU:1, one launch (start us, length us, event | category | flops | bytes accessed | tf_op | source)
XLA Modules:
  0.0 263.8 jit_solution(6888572505952773997)
XLA Ops:
  0.6 2.2 broadcast_in_dim.67
  2.8 9.1 %all-to-all-start = ((bf16[8,72,1024]{2,1,0:T(8,128)(2,1)}), bf16[8,72,1024]{2,1,0:T(8,128)(2,1)S(1)}, u32[]{:S(2)}, u32[]{:S(2)}) async-start(bf16[8,72,1024]{2,1,0:T(8,128)(2,1)} %broadcast_in_dim.67), calls=%async_computation | async-start | bytes 2359296 | tf_op jit(solution)/shard_map/all_to_all | solution.py:366
  13.0 1.5 collective-permute-start.11
  14.5 1.2 collective-permute-start.12
  16.6 1.5 collective-permute-start.3
  20.3 23.8 %all-to-all-done = bf16[8,72,1024]{2,1,0:T(8,128)(2,1)S(1)} async-done(((bf16[8,72,1024]{2,1,0:T(8,128)(2,1)}), bf16[8,72,1024]{2,1,0:T(8,128)(2,1)S(1)}, u32[]{:S(2)}, u32[]{:S(2)}) %all-to-all-start) | async-done | bytes 1179680 | tf_op jit(solution)/shard_map/all_to_all | solution.py:366
  46.0 2.1 fusion.1
  49.1 3.5 %hidden_products.5 = (f32[512,256]{1,0:T(8,128)}, bf16[512,256]{1,0:T(8,128)(2,1)}) custom-call(s32[1]{0:T(128)} %bitcast.place_ref, bf16[256,2048]{1,0:T(8,128)(2,1)} %own_ref.9, bf16[256,2048]{1,0:T(8,128)(2,1)} %copy-done.1, bf16[256,1024]{1,0:T(8,128)(2,1)} %get-tuple-element.135.refs_0_, bf16[256,1024]{1,0:T(8,128)(2,1)} %get-tuple-element.134.refs_1_.refs_0_), custom_call_target="tpu_custom_call" | custom-call | flops 536870912 | bytes 1048576 | tf_op jit(solution)/shard_map/hidden_products/pallas_call | solution.py:93
  52.6 18.4 %collective-permute-done.9 = bf16[8,72,1024]{2,1,0:T(8,128)(2,1)} collective-permute-done((bf16[8,72,1024]{2,1,0:T(8,128)(2,1)S(1)}, bf16[8,72,1024]{2,1,0:T(8,128)(2,1)}, u32[]{:S(2)}, u32[]{:S(2)}) %collective-permute-start.9) | collective-permute-done | bytes 1179680 | tf_op jit(solution)/shard_map/ppermute | solution.py:29
  71.0 3.1 %fusion.19 = (bf16[8,1,2,72,1024]{4,3,2,1,0:T(8,128)(2,1)S(1)}, bf16[8,2,72,1024]{3,2,1,0:T(8,128)(2,1)}) fusion(bf16[8,1,72,1024]{3,2,1,0:T(8,128)(2,1)} %bitcast.18, bf16[8,1,72,1024]{3,2,1,0:T(8,128)(2,1)S(1)} %bitcast.48), kind=kLoop, calls=%fused_computation.71 | loop fusion | flops 1179648 | bytes 7077888 | tf_op jit(solution)/shard_map/stack | solution.py:434
  74.1 1.5 collective-permute-start.10
  82.4 1.3 copy.77
  88.7 1.5 collective-permute-start.16
  90.2 4.7 %collective-permute-done.4 = bf16[1032,256]{1,0:T(8,128)(2,1)S(1)} collective-permute-done((bf16[1032,256]{1,0:T(8,128)(2,1)}, bf16[1032,256]{1,0:T(8,128)(2,1)S(1)}, u32[]{:S(2)}, u32[]{:S(2)}) %collective-permute-start.4) | collective-permute-done | bytes 528416 | tf_op jit(solution)/shard_map/ppermute | solution.py:29
  99.2 2.3 copy.58
  101.5 1.9 constant_dynamic-slice_fusion
  103.4 2.1 copy.59
  105.6 1.5 collective-permute-start.5
  107.2 1.2 collective-permute-start.6
  108.4 4.6 %hidden_products.6 = (f32[512,512]{1,0:T(8,128)}, bf16[512,512]{1,0:T(8,128)(2,1)}) custom-call(s32[1]{0:T(128)} %bitcast.place_ref, bf16[256,2048]{1,0:T(8,128)(2,1)} %own_ref.9, bf16[256,2048]{1,0:T(8,128)(2,1)} %copy-done.1, bf16[256,1024]{1,0:T(8,128)(2,1)} %collective-permute-done.1.refs_0_.refs_7_, bf16[256,1024]{1,0:T(8,128)(2,1)} %collective-permute-done.2.refs_1_, ...), custom_call_target="tpu_custom_call" | custom-call | flops 1073741824 | bytes 2097152 | tf_op jit(solution)/shard_map/hidden_products/pallas_call | solution.py:93
  113.0 1.3 collective-permute-start.13
  115.7 4.2 %collective-permute-done.5.refs_0_.refs_6_ = bf16[256,1024]{1,0:T(8,128)(2,1)} collective-permute-done((bf16[256,1024]{1,0:T(8,128)(2,1)}, bf16[256,1024]{1,0:T(8,128)(2,1)}, u32[]{:S(2)}, u32[]{:S(2)}) %collective-permute-start.5) | collective-permute-done | bytes 524320 | tf_op jit(solution)/shard_map/ppermute | solution.py:39
  120.0 4.8 %collective-permute-done.6.refs_1_.refs_2_ = bf16[256,1024]{1,0:T(8,128)(2,1)} collective-permute-done((bf16[256,1024]{1,0:T(8,128)(2,1)}, bf16[256,1024]{1,0:T(8,128)(2,1)}, u32[]{:S(2)}, u32[]{:S(2)}) %collective-permute-start.6) | collective-permute-done | bytes 524320 | tf_op jit(solution)/shard_map/ppermute | solution.py:39
  124.7 2.7 %collective-permute-start.8 = (bf16[256,1024]{1,0:T(8,128)(2,1)}, bf16[256,1024]{1,0:T(8,128)(2,1)}, u32[]{:S(2)}, u32[]{:S(2)}) collective-permute-start(bf16[256,1024]{1,0:T(8,128)(2,1)} %collective-permute-done.6.refs_1_.refs_2_), channel_id=1, source_target_pairs={{0,224},{32,0},{64,32},{96,64},{128,96},{160,128},{192,160},{224,1... | collective-permute-start | bytes 1572872 | tf_op jit(solution)/shard_map/ppermute | solution.py:39
  127.4 4.3 %pad_maximum_fusion = bf16[8,2,2,72,1024]{4,3,2,1,0:T(8,128)(2,1)} fusion(bf16[8,1,2,72,1024]{4,3,2,1,0:T(8,128)(2,1)} %bitcast.21, bf16[8,1,2,72,1024]{4,3,2,1,0:T(8,128)(2,1)S(1)} %get-tuple-element.130), kind=kLoop, calls=%fused_computation | loop fusion | flops 2359296 | bytes 9437184 | tf_op jit(solution)/shard_map/stack | solution.py:434
  131.7 2.4 collective-permute-start.14
  134.2 16.4 %forward.1 = (bf16[2048,512]{1,0:T(8,128)(2,1)}, bf16[2048,512]{1,0:T(8,128)(2,1)}, bf16[512,2048]{1,0:T(8,128)(2,1)}, f32[512,2048]{1,0:T(8,128)}) custom-call(s32[8]{0:T(128)} %copy-done.18, s32[8]{0:T(128)} %fusion.17.window_ref, s32[4]{0:T(128)} %copy-done.17, s32[1]{0:T(128)} %bitcast.14.core_ref, bf16[8,288,1024]{2,1,0:T(8,128)(2,1)} %bitcast.49, ...), custom_call_target="tpu_custom_call" | custom-call | flops 4563402752 | bytes 20971520 | tf_op jit(solution)/shard_map/forward/pallas_call | solution.py:160
  150.7 4.7 %hidden_products.7 = (f32[512,512]{1,0:T(8,128)}, bf16[512,512]{1,0:T(8,128)(2,1)}) custom-call(s32[1]{0:T(128)} %bitcast.place_ref, bf16[256,2048]{1,0:T(8,128)(2,1)} %own_ref.9, bf16[256,2048]{1,0:T(8,128)(2,1)} %copy-done.1, bf16[256,1024]{1,0:T(8,128)(2,1)} %collective-permute-done.5.refs_0_.refs_6_, ...), custom_call_target="tpu_custom_call" | custom-call | flops 1073741824 | bytes 2097152 | tf_op jit(solution)/shard_map/hidden_products/pallas_call | solution.py:93
  156.4 4.7 %hidden_products.8 = (f32[512,512]{1,0:T(8,128)}, bf16[512,512]{1,0:T(8,128)(2,1)}) custom-call(s32[1]{0:T(128)} %bitcast.place_ref, bf16[256,2048]{1,0:T(8,128)(2,1)} %own_ref.9, bf16[256,2048]{1,0:T(8,128)(2,1)} %copy-done.1, bf16[256,1024]{1,0:T(8,128)(2,1)} %collective-permute-done.7.refs_0_.refs_5_, ...), custom_call_target="tpu_custom_call" | custom-call | flops 1073741824 | bytes 2097152 | tf_op jit(solution)/shard_map/hidden_products/pallas_call | solution.py:93
  161.7 3.9 %collective-permute-done.15.refs_4_.refs_0_ = bf16[256,1024]{1,0:T(8,128)(2,1)S(1)} collective-permute-done((bf16[256,1024]{1,0:T(8,128)(2,1)}, bf16[256,1024]{1,0:T(8,128)(2,1)S(1)}, u32[]{:S(2)}, u32[]{:S(2)}) %collective-permute-start.15) | collective-permute-done | bytes 524320 | tf_op jit(solution)/shard_map/ppermute | solution.py:39
  166.4 5.9 %summed_product.2 = bf16[512,1024]{1,0:T(8,128)(2,1)} custom-call(bf16[512,2048]{1,0:T(8,128)(2,1)} %get-tuple-element.105.left_ref, bf16[256,1024]{1,0:T(8,128)(2,1)} %get-tuple-element.135.refs_0_, bf16[256,1024]{1,0:T(8,128)(2,1)} %collective-permute-done.2.refs_1_, bf16[256,1024]{1,0:T(8,128)(2,1)} %collective-permute-done.6.refs_1_.refs_2_, ...), custom_call_target="tpu_custom_call" | custom-call | flops 2147483648 | bytes 10485760 | tf_op jit(solution)/shard_map/summed_product/pallas_call | solution.py:60
  172.3 6.6 %all-to-all-start.1 = ((bf16[16,32,1024]{2,1,0:T(8,128)(2,1)}), bf16[16,32,1024]{2,1,0:T(8,128)(2,1)S(1)}, u32[]{:S(2)}, u32[]{:S(2)}) async-start(bf16[16,32,1024]{2,1,0:T(8,128)(2,1)} %bitcast.56), calls=%async_computation.1 | async-start | bytes 2097152 | tf_op jit(solution)/shard_map/all_to_all | solution.py:464
  179.8 8.4 %input_products.1 = (f32[512,512]{1,0:T(8,128)}, f32[512,512]{1,0:T(8,128)}, f32[8,512]{1,0:T(8,128)}) custom-call(f32[512,512]{1,0:T(8,128)} %get-tuple-element.98.refs_0_, f32[512,512]{1,0:T(8,128)} %get-tuple-element.99.refs_1_, f32[512,512]{1,0:T(8,128)} %get-tuple-element.100.refs_2_, f32[512,256]{1,0:T(8,128)} %get-tuple-element.101.refs_3_, ...), custom_call_target="tpu_custom_call" | custom-call | flops 1879048192 | bytes 8388608 | tf_op jit(solution)/shard_map/input_products/pallas_call | solution.py:243
  188.3 3.1 %collective-permute-done.20.refs_1_.refs_4_ = bf16[256,1024]{1,0:T(8,128)(2,1)S(1)} collective-permute-done((bf16[256,1024]{1,0:T(8,128)(2,1)S(1)}, bf16[256,1024]{1,0:T(8,128)(2,1)S(1)}, u32[]{:S(2)}, u32[]{:S(2)}) %collective-permute-start.20) | collective-permute-done | bytes 524320 | tf_op jit(solution)/shard_map/ppermute | solution.py:39
  192.2 3.5 %hidden_products.9 = (f32[512,256]{1,0:T(8,128)}, bf16[512,256]{1,0:T(8,128)(2,1)}) custom-call(s32[1]{0:T(128)} %bitcast.place_ref, bf16[256,2048]{1,0:T(8,128)(2,1)} %own_ref.9, bf16[256,2048]{1,0:T(8,128)(2,1)} %copy-done.1, bf16[256,1024]{1,0:T(8,128)(2,1)} %copy-done.9, bf16[256,1024]{1,0:T(8,128)(2,1)} %copy-done.8), custom_call_target="tpu_custom_call" | custom-call | flops 536870912 | bytes 1048576 | tf_op jit(solution)/shard_map/hidden_products/pallas_call | solution.py:93
  195.6 2.0 collective-permute-start.23
  197.6 1.4 collective-permute-done.23.other_ref
  199.7 4.1 %input_pieces.1 = bf16[16,96,256]{2,1,0:T(8,128)(2,1)} custom-call(f32[512,256]{1,0:T(8,128)} %get-tuple-element.116.part_ref, bf16[512,256]{1,0:T(8,128)(2,1)} %copy-done.12, f32[512,2048]{1,0:T(8,128)} %get-tuple-element.109.refs_8_.slope_ref, bf16[2048,512]{1,0:T(8,128)(2,1)} %get-tuple-element.110.refs_9_.in_ref, ...), custom_call_target="tpu_custom_call" | custom-call | flops 268435456 | bytes 1048576 | tf_op jit(solution)/shard_map/input_pieces/pallas_call | solution.py:315
  203.8 6.7 %all-to-all-start.2 = ((bf16[16,96,256]{2,1,0:T(8,128)(2,1)}), bf16[16,96,256]{2,1,0:T(8,128)(2,1)S(1)}, u32[]{:S(2)}, u32[]{:S(2)}) async-start(bf16[16,96,256]{2,1,0:T(8,128)(2,1)} %input_pieces.1), calls=%async_computation.2 | async-start | bytes 1572864 | tf_op jit(solution)/shard_map/all_to_all | solution.py:474
  210.7 6.0 %summed_product.3 = bf16[512,1024]{1,0:T(8,128)(2,1)} custom-call(bf16[512,2048]{1,0:T(8,128)(2,1)} %get-tuple-element.105.left_ref, bf16[256,1024]{1,0:T(8,128)(2,1)} %get-tuple-element.134.refs_1_.refs_0_, bf16[256,1024]{1,0:T(8,128)(2,1)} %collective-permute-done.12.refs_3_.refs_1_, bf16[256,1024]{1,0:T(8,128)(2,1)} %collective-permute-done.17.refs_3_.refs_2_, ...), custom_call_target="tpu_custom_call" | custom-call | flops 2147483648 | bytes 10485760 | tf_op jit(solution)/shard_map/summed_product/pallas_call | solution.py:60
  216.7 6.2 %all-to-all-done.2 = bf16[16,96,256]{2,1,0:T(8,128)(2,1)S(1)} async-done(((bf16[16,96,256]{2,1,0:T(8,128)(2,1)}), bf16[16,96,256]{2,1,0:T(8,128)(2,1)S(1)}, u32[]{:S(2)}, u32[]{:S(2)}) %all-to-all-start.2) | async-done | bytes 786464 | tf_op jit(solution)/shard_map/all_to_all | solution.py:474
  223.3 2.8 %collective-permute-done.24 = f32[28,256]{1,0:T(8,128)S(1)} collective-permute-done((f32[28,256]{1,0:T(8,128)S(1)}, f32[28,256]{1,0:T(8,128)S(1)}, u32[]{:S(2)}, u32[]{:S(2)}) %collective-permute-start.24) | collective-permute-done | bytes 28704 | tf_op jit(solution)/shard_map/ppermute | solution.py:494
  226.1 3.7 %collective-permute-done.25 = f32[28,256]{1,0:T(8,128)S(1)} collective-permute-done((f32[28,256]{1,0:T(8,128)S(1)}, f32[28,256]{1,0:T(8,128)S(1)}, u32[]{:S(2)}, u32[]{:S(2)}) %collective-permute-start.25) | collective-permute-done | bytes 28704 | tf_op jit(solution)/shard_map/ppermute | solution.py:494
  229.9 2.2 collective-permute-start.26
  232.0 4.5 %collective-permute-done.26 = f32[28,256]{1,0:T(8,128)S(1)} collective-permute-done((f32[28,256]{1,0:T(8,128)S(1)}, f32[28,256]{1,0:T(8,128)S(1)}, u32[]{:S(2)}, u32[]{:S(2)}) %collective-permute-start.26) | collective-permute-done | bytes 28704 | tf_op jit(solution)/shard_map/ppermute | solution.py:494
  236.5 5.6 %collective-permute-start.27 = (f32[28,256]{1,0:T(8,128)S(1)}, f32[28,256]{1,0:T(8,128)S(1)}, u32[]{:S(2)}, u32[]{:S(2)}) collective-permute-start(f32[28,256]{1,0:T(8,128)S(1)} %add.94), channel_id=1, source_target_pairs={{0,1},{1,0},{2,3},{3,2},{4,5},{5,4},{6,7},{7,6},{8,9},{9,8},{10,11... | collective-permute-start | bytes 86024 | tf_op jit(solution)/shard_map/ppermute | solution.py:29
  243.0 3.7 %all-to-all-start.3 = ((bf16[16,32,1024]{2,1,0:T(8,128)(2,1)}), bf16[16,32,1024]{2,1,0:T(8,128)(2,1)S(1)}, u32[]{:S(2)}, u32[]{:S(2)}) async-start(bf16[16,32,1024]{2,1,0:T(8,128)(2,1)} %bitcast.26), calls=%async_computation.3 | async-start | bytes 2097152 | tf_op jit(solution)/shard_map/all_to_all | solution.py:476
  249.7 13.2 %all-to-all-done.3 = bf16[16,32,1024]{2,1,0:T(8,128)(2,1)S(1)} async-done(((bf16[16,32,1024]{2,1,0:T(8,128)(2,1)}), bf16[16,32,1024]{2,1,0:T(8,128)(2,1)S(1)}, u32[]{:S(2)}, u32[]{:S(2)}) %all-to-all-start.3) | async-done | bytes 1048608 | tf_op jit(solution)/shard_map/all_to_all | solution.py:476
  (147 shorter events, 34.7 us)
Async XLA Ops:
  0.6 11.3 %copy-start.4 = (bf16[1,256,2048]{2,1,0:T(8,128)(2,1)S(1)}, bf16[1,256,2048]{2,1,0:T(8,128)(2,1)}, u32[]{:S(2)}) copy-start(bf16[1,256,2048]{2,1,0:T(8,128)(2,1)} %param.15) | copy-start | bytes 3145732
  2.8 12.9 %copy-start.13 = (bf16[512,256]{1,0:T(8,128)(2,1)S(1)}, bf16[512,256]{1,0:T(8,128)(2,1)}, u32[]{:S(2)}) copy-start(bf16[512,256]{1,0:T(8,128)(2,1)} %param.12) | copy-start | bytes 786436
  2.8 15.3 %copy-start = (bf16[256,2048]{1,0:T(8,128)(2,1)S(1)}, bf16[256,2048]{1,0:T(8,128)(2,1)}, u32[]{:S(2)}) copy-start(bf16[256,2048]{1,0:T(8,128)(2,1)} %own_ref.9) | copy-start | bytes 3145732
  2.8 16.5 %copy-start.14 = (s32[1,2304]{1,0:T(1,128)S(1)}, s32[1,2304]{1,0:T(1,128)}, u32[]{:S(2)}) copy-start(s32[1,2304]{1,0:T(1,128)} %param.17) | copy-start | bytes 27652
  2.8 16.5 %copy-start.15 = (s32[1,2]{1,0:T(1,128)S(1)}, s32[1,2]{1,0:T(1,128)}, u32[]{:S(2)}) copy-start(s32[1,2]{1,0:T(1,128)} %param.16) | copy-start | bytes 28
  2.8 41.2 %all-to-all-start = ((bf16[8,72,1024]{2,1,0:T(8,128)(2,1)}), bf16[8,72,1024]{2,1,0:T(8,128)(2,1)S(1)}, u32[]{:S(2)}, u32[]{:S(2)}) async-start(bf16[8,72,1024]{2,1,0:T(8,128)(2,1)} %broadcast_in_dim.67), calls=%async_computation | async-start | bytes 2359296 | tf_op jit(solution)/shard_map/all_to_all | solution.py:366
  13.0 75.7 %collective-permute-start.11 = (bf16[256,1024]{1,0:T(8,128)(2,1)}, bf16[256,1024]{1,0:T(8,128)(2,1)}, u32[]{:S(2)}, u32[]{:S(2)}) collective-permute-start(bf16[256,1024]{1,0:T(8,128)(2,1)} %get-tuple-element.134.refs_1_.refs_0_), channel_id=1, source_target_pairs={{0,32},{32,64},{64,96},{96,128},{128,160},{160,192},{192,224},{224... | collective-permute-start | bytes 1572872 | tf_op jit(solution)/shard_map/ppermute | solution.py:39
  14.5 74.2 %collective-permute-start.12 = (bf16[256,1024]{1,0:T(8,128)(2,1)}, bf16[256,1024]{1,0:T(8,128)(2,1)}, u32[]{:S(2)}, u32[]{:S(2)}) collective-permute-start(bf16[256,1024]{1,0:T(8,128)(2,1)} %get-tuple-element.134.refs_1_.refs_0_), channel_id=1, source_target_pairs={{0,224},{32,0},{64,32},{96,64},{128,96},{160,128},{192,160},{224,1... | collective-permute-start | bytes 1572872 | tf_op jit(solution)/shard_map/ppermute | solution.py:39
  16.6 60.6 %collective-permute-start.3 = (bf16[512,256]{0,1:T(8,128)(2,1)}, bf16[512,256]{0,1:T(8,128)(2,1)}, u32[]{:S(2)}, u32[]{:S(2)}) collective-permute-start(bf16[512,256]{0,1:T(8,128)(2,1)} %copy.50), channel_id=1, source_target_pairs={{0,1},{1,0},{2,3},{3,2},{4,5},{5,4},{6,7},{7,6},{8,9},{9,8},{10,11... | collective-permute-start | bytes 786440 | tf_op jit(solution)/shard_map/ppermute | solution.py:29
  18.1 30.0 %collective-permute-start = (bf16[256,2048]{1,0:T(8,128)(2,1)S(1)}, bf16[256,2048]{1,0:T(8,128)(2,1)S(1)}, u32[]{:S(2)}, u32[]{:S(2)}) collective-permute-start(bf16[256,2048]{1,0:T(8,128)(2,1)S(1)} %copy-done), channel_id=1, source_target_pairs={{0,16},{16,0},{1,17},{17,1},{2,18},{18,2},{3,19},{19,3},{4,20},{20... | collective-permute-start | bytes 3145736 | tf_op jit(solution)/shard_map/ppermute | solution.py:29
  20.1 25.2 %copy-start.18 = (s32[8]{0:T(128)}, s32[8]{0:T(128)S(1)}, u32[]{:S(2)}) copy-start(s32[8]{0:T(128)S(1)} %fusion.16.base_ref) | copy-start | bytes 100
  44.0 27.0 %collective-permute-start.9 = (bf16[8,72,1024]{2,1,0:T(8,128)(2,1)S(1)}, bf16[8,72,1024]{2,1,0:T(8,128)(2,1)}, u32[]{:S(2)}, u32[]{:S(2)}) collective-permute-start(bf16[8,72,1024]{2,1,0:T(8,128)(2,1)S(1)} %all-to-all-done), channel_id=1, source_target_pairs={{0,16},{16,0},{1,17},{17,1},{2,18},{18,2},{3,19},{19,3},{4,20},{20... | collective-permute-start | bytes 3538952 | tf_op jit(solution)/shard_map/ppermute | solution.py:29
  48.1 1.0 copy-start.1
  48.1 57.5 %collective-permute-start.1 = (bf16[256,1024]{1,0:T(8,128)(2,1)}, bf16[256,1024]{1,0:T(8,128)(2,1)}, u32[]{:S(2)}, u32[]{:S(2)}) collective-permute-start(bf16[256,1024]{1,0:T(8,128)(2,1)} %get-tuple-element.135.refs_0_), channel_id=1, source_target_pairs={{0,32},{32,64},{64,96},{96,128},{128,160},{160,192},{192,224},{224... | collective-permute-start | bytes 1572872 | tf_op jit(solution)/shard_map/ppermute | solution.py:39
  71.0 4.6 %copy-start.16 = (f32[256]{0:T(256)S(1)}, f32[256]{0:T(256)}, u32[]{:S(2)}) copy-start(f32[256]{0:T(256)} %param.13) | copy-start | bytes 3076
  74.1 50.6 %collective-permute-start.10 = (bf16[8,2,72,1024]{3,2,1,0:T(8,128)(2,1)}, bf16[8,2,72,1024]{3,2,1,0:T(8,128)(2,1)}, u32[]{:S(2)}, u32[]{:S(2)}) collective-permute-start(bf16[8,2,72,1024]{3,2,1,0:T(8,128)(2,1)} %get-tuple-element.131), channel_id=1, source_target_pairs={{0,1},{1,0},{2,3},{3,2},{4,5},{5,4},{6,7},{7,6},{8,9},{9,8},{10,11... | collective-permute-start | bytes 7077896 | tf_op jit(solution)/shard_map/ppermute | solution.py:29
  81.0 13.9 %collective-permute-start.4 = (bf16[1032,256]{1,0:T(8,128)(2,1)}, bf16[1032,256]{1,0:T(8,128)(2,1)S(1)}, u32[]{:S(2)}, u32[]{:S(2)}) collective-permute-start(bf16[1032,256]{1,0:T(8,128)(2,1)} %copy.55), channel_id=1, source_target_pairs={{0,16},{16,0},{1,17},{17,1},{2,18},{18,2},{3,19},{19,3},{4,20},{20... | collective-permute-start | bytes 1585160 | tf_op jit(solution)/shard_map/ppermute | solution.py:29
  88.7 16.9 %collective-permute-start.2 = (bf16[256,1024]{1,0:T(8,128)(2,1)}, bf16[256,1024]{1,0:T(8,128)(2,1)}, u32[]{:S(2)}, u32[]{:S(2)}) collective-permute-start(bf16[256,1024]{1,0:T(8,128)(2,1)} %get-tuple-element.135.refs_0_), channel_id=1, source_target_pairs={{0,224},{32,0},{64,32},{96,64},{128,96},{160,128},{192,160},{224,1... | collective-permute-start | bytes 1572872 | tf_op jit(solution)/shard_map/ppermute | solution.py:39
  88.7 24.3 %collective-permute-start.16 = (bf16[256,1024]{1,0:T(8,128)(2,1)}, bf16[256,1024]{1,0:T(8,128)(2,1)}, u32[]{:S(2)}, u32[]{:S(2)}) collective-permute-start(bf16[256,1024]{1,0:T(8,128)(2,1)} %collective-permute-done.11.refs_2_.refs_7_), channel_id=1, source_target_pairs={{0,32},{32,64},{64,96},{96,128},{128,160},{160,192},{192,224},{224... | collective-permute-start | bytes 1572872 | tf_op jit(solution)/shard_map/ppermute | solution.py:39
  94.9 20.3 %collective-permute-start.17 = (bf16[256,1024]{1,0:T(8,128)(2,1)}, bf16[256,1024]{1,0:T(8,128)(2,1)}, u32[]{:S(2)}, u32[]{:S(2)}) collective-permute-start(bf16[256,1024]{1,0:T(8,128)(2,1)} %collective-permute-done.12.refs_3_.refs_1_), channel_id=1, source_target_pairs={{0,224},{32,0},{64,32},{96,64},{128,96},{160,128},{192,160},{224,1... | collective-permute-start | bytes 1572872 | tf_op jit(solution)/shard_map/ppermute | solution.py:39
  97.2 0.8 copy-start.2
  99.2 6.3 %copy-start.3 = (bf16[1032,256]{0,1:T(8,128)(2,1)S(1)}, bf16[1032,256]{0,1:T(8,128)(2,1)}, u32[]{:S(2)}) copy-start(bf16[1032,256]{0,1:T(8,128)(2,1)} %copy-done.2) | copy-start | bytes 1585156
  105.6 14.3 %collective-permute-start.5 = (bf16[256,1024]{1,0:T(8,128)(2,1)}, bf16[256,1024]{1,0:T(8,128)(2,1)}, u32[]{:S(2)}, u32[]{:S(2)}) collective-permute-start(bf16[256,1024]{1,0:T(8,128)(2,1)} %collective-permute-done.1.refs_0_.refs_7_), channel_id=1, source_target_pairs={{0,32},{32,64},{64,96},{96,128},{128,160},{160,192},{192,224},{224... | collective-permute-start | bytes 1572872 | tf_op jit(solution)/shard_map/ppermute | solution.py:39
  107.2 17.6 %collective-permute-start.6 = (bf16[256,1024]{1,0:T(8,128)(2,1)}, bf16[256,1024]{1,0:T(8,128)(2,1)}, u32[]{:S(2)}, u32[]{:S(2)}) collective-permute-start(bf16[256,1024]{1,0:T(8,128)(2,1)} %collective-permute-done.2.refs_1_), channel_id=1, source_target_pairs={{0,224},{32,0},{64,32},{96,64},{128,96},{160,128},{192,160},{224,1... | collective-permute-start | bytes 1572872 | tf_op jit(solution)/shard_map/ppermute | solution.py:39
  113.0 18.7 %collective-permute-start.13 = (bf16[512,512]{1,0:T(8,128)(2,1)}, bf16[512,512]{1,0:T(8,128)(2,1)}, u32[]{:S(2)}, u32[]{:S(2)}) collective-permute-start(bf16[512,512]{1,0:T(8,128)(2,1)} %get-tuple-element.85), channel_id=1, source_target_pairs={{0,1},{1,0},{2,3},{3,2},{4,5},{5,4},{6,7},{7,6},{8,9},{9,8},{10,11... | collective-permute-start | bytes 1572872 | tf_op jit(solution)/shard_map/ppermute | solution.py:29
  115.2 40.2 %collective-permute-start.18 = (bf16[256,1024]{1,0:T(8,128)(2,1)}, bf16[256,1024]{1,0:T(8,128)(2,1)S(1)}, u32[]{:S(2)}, u32[]{:S(2)}) collective-permute-start(bf16[256,1024]{1,0:T(8,128)(2,1)} %collective-permute-done.16.refs_2_.refs_6_), channel_id=1, source_target_pairs={{0,32},{32,64},{64,96},{96,128},{128,160},{160,192},{192,224},{224... | collective-permute-start | bytes 1572872 | tf_op jit(solution)/shard_map/ppermute | solution.py:39
  119.9 35.5 %collective-permute-start.19 = (bf16[256,1024]{1,0:T(8,128)(2,1)}, bf16[256,1024]{1,0:T(8,128)(2,1)S(1)}, u32[]{:S(2)}, u32[]{:S(2)}) collective-permute-start(bf16[256,1024]{1,0:T(8,128)(2,1)} %collective-permute-done.17.refs_3_.refs_2_), channel_id=1, source_target_pairs={{0,224},{32,0},{64,32},{96,64},{128,96},{160,128},{192,160},{224,1... | collective-permute-start | bytes 1572872 | tf_op jit(solution)/shard_map/ppermute | solution.py:39
  124.7 25.8 %collective-permute-start.7 = (bf16[256,1024]{1,0:T(8,128)(2,1)}, bf16[256,1024]{1,0:T(8,128)(2,1)}, u32[]{:S(2)}, u32[]{:S(2)}) collective-permute-start(bf16[256,1024]{1,0:T(8,128)(2,1)} %collective-permute-done.5.refs_0_.refs_6_), channel_id=1, source_target_pairs={{0,32},{32,64},{64,96},{96,128},{128,160},{160,192},{192,224},{224... | collective-permute-start | bytes 1572872 | tf_op jit(solution)/shard_map/ppermute | solution.py:39
  124.7 25.8 %collective-permute-start.8 = (bf16[256,1024]{1,0:T(8,128)(2,1)}, bf16[256,1024]{1,0:T(8,128)(2,1)}, u32[]{:S(2)}, u32[]{:S(2)}) collective-permute-start(bf16[256,1024]{1,0:T(8,128)(2,1)} %collective-permute-done.6.refs_1_.refs_2_), channel_id=1, source_target_pairs={{0,224},{32,0},{64,32},{96,64},{128,96},{160,128},{192,160},{224,1... | collective-permute-start | bytes 1572872 | tf_op jit(solution)/shard_map/ppermute | solution.py:39
  131.7 18.9 %collective-permute-start.14 = (bf16[512,256]{1,0:T(8,128)(2,1)}, bf16[512,256]{1,0:T(8,128)(2,1)S(1)}, u32[]{:S(2)}, u32[]{:S(2)}) collective-permute-start(bf16[512,256]{1,0:T(8,128)(2,1)} %get-tuple-element.86), channel_id=1, source_target_pairs={{0,1},{1,0},{2,3},{3,2},{4,5},{5,4},{6,7},{7,6},{8,9},{9,8},{10,11... | collective-permute-start | bytes 786440 | tf_op jit(solution)/shard_map/ppermute | solution.py:29
  150.6 4.8 %copy-start.11 = (bf16[512,256]{1,0:T(8,128)(2,1)}, bf16[512,256]{1,0:T(8,128)(2,1)S(1)}, u32[]{:S(2)}) copy-start(bf16[512,256]{1,0:T(8,128)(2,1)S(1)} %collective-permute-done.14.refs_7_) | copy-start | bytes 786436
  150.6 15.0 %collective-permute-start.15 = (bf16[256,1024]{1,0:T(8,128)(2,1)}, bf16[256,1024]{1,0:T(8,128)(2,1)S(1)}, u32[]{:S(2)}, u32[]{:S(2)}) collective-permute-start(bf16[256,1024]{1,0:T(8,128)(2,1)} %collective-permute-done.7.refs_0_.refs_5_), channel_id=1, source_target_pairs={{0,32},{32,64},{64,96},{96,128},{128,160},{160,192},{192,224},{224... | collective-permute-start | bytes 1572872 | tf_op jit(solution)/shard_map/ppermute | solution.py:39
  155.4 23.6 %collective-permute-start.21 = (bf16[512,512]{1,0:T(8,128)(2,1)}, bf16[512,512]{1,0:T(8,128)(2,1)}, u32[]{:S(2)}, u32[]{:S(2)}) collective-permute-start(bf16[512,512]{1,0:T(8,128)(2,1)} %get-tuple-element.103), channel_id=1, source_target_pairs={{0,1},{1,0},{2,3},{3,2},{4,5},{5,4},{6,7},{7,6},{8,9},{9,8},{10,11... | collective-permute-start | bytes 1572872 | tf_op jit(solution)/shard_map/ppermute | solution.py:29
  155.4 0.8 copy-start.5
  155.4 1.0 copy-start.6
  161.2 17.8 %collective-permute-start.22 = (bf16[512,512]{1,0:T(8,128)(2,1)}, bf16[512,512]{1,0:T(8,128)(2,1)S(1)}, u32[]{:S(2)}, u32[]{:S(2)}) collective-permute-start(bf16[512,512]{1,0:T(8,128)(2,1)} %get-tuple-element.96), channel_id=1, source_target_pairs={{0,1},{1,0},{2,3},{3,2},{4,5},{5,4},{6,7},{7,6},{8,9},{9,8},{10,11... | collective-permute-start | bytes 1572872 | tf_op jit(solution)/shard_map/ppermute | solution.py:29
  165.6 0.8 copy-start.9
  172.3 6.6 %copy-start.7 = (bf16[256,1024]{1,0:T(8,128)(2,1)S(1)}, bf16[256,1024]{1,0:T(8,128)(2,1)}, u32[]{:S(2)}) copy-start(bf16[256,1024]{1,0:T(8,128)(2,1)} %copy-done.6) | copy-start | bytes 1572868
  172.3 31.5 %all-to-all-start.1 = ((bf16[16,32,1024]{2,1,0:T(8,128)(2,1)}), bf16[16,32,1024]{2,1,0:T(8,128)(2,1)S(1)}, u32[]{:S(2)}, u32[]{:S(2)}) async-start(bf16[16,32,1024]{2,1,0:T(8,128)(2,1)} %bitcast.56), calls=%async_computation.1 | async-start | bytes 2097152 | tf_op jit(solution)/shard_map/all_to_all | solution.py:464
  178.9 12.4 %collective-permute-start.20 = (bf16[256,1024]{1,0:T(8,128)(2,1)S(1)}, bf16[256,1024]{1,0:T(8,128)(2,1)S(1)}, u32[]{:S(2)}, u32[]{:S(2)}) collective-permute-start(bf16[256,1024]{1,0:T(8,128)(2,1)S(1)} %copy-done.7), channel_id=1, source_target_pairs={{0,224},{32,0},{64,32},{96,64},{128,96},{160,128},{192,160},{224,1... | collective-permute-start | bytes 1572872 | tf_op jit(solution)/shard_map/ppermute | solution.py:39
  191.3 0.8 copy-start.8
  195.6 3.4 %collective-permute-start.23 = (bf16[512,256]{1,0:T(8,128)(2,1)}, bf16[512,256]{1,0:T(8,128)(2,1)S(1)}, u32[]{:S(2)}, u32[]{:S(2)}) collective-permute-start(bf16[512,256]{1,0:T(8,128)(2,1)} %get-tuple-element.117), channel_id=1, source_target_pairs={{0,1},{1,0},{2,3},{3,2},{4,5},{5,4},{6,7},{7,6},{8,9},{9,8},{10,11... | collective-permute-start | bytes 786440 | tf_op jit(solution)/shard_map/ppermute | solution.py:29
  203.8 19.1 %all-to-all-start.2 = ((bf16[16,96,256]{2,1,0:T(8,128)(2,1)}), bf16[16,96,256]{2,1,0:T(8,128)(2,1)S(1)}, u32[]{:S(2)}, u32[]{:S(2)}) async-start(bf16[16,96,256]{2,1,0:T(8,128)(2,1)} %input_pieces.1), calls=%async_computation.2 | async-start | bytes 1572864 | tf_op jit(solution)/shard_map/all_to_all | solution.py:474
  223.2 2.9 %collective-permute-start.24 = (f32[28,256]{1,0:T(8,128)S(1)}, f32[28,256]{1,0:T(8,128)S(1)}, u32[]{:S(2)}, u32[]{:S(2)}) collective-permute-start(f32[28,256]{1,0:T(8,128)S(1)} %pad_maximum_fusion.4), channel_id=1, source_target_pairs={{0,32},{32,0},{64,96},{96,64},{128,160},{160,128},{192,224},{224,1... | collective-permute-start | bytes 86024 | tf_op jit(solution)/shard_map/ppermute | solution.py:494
  226.0 3.8 %collective-permute-start.25 = (f32[28,256]{1,0:T(8,128)S(1)}, f32[28,256]{1,0:T(8,128)S(1)}, u32[]{:S(2)}, u32[]{:S(2)}) collective-permute-start(f32[28,256]{1,0:T(8,128)S(1)} %fusion.18), channel_id=1, source_target_pairs={{0,64},{32,96},{64,0},{96,32},{128,192},{160,224},{192,128},{224,1... | collective-permute-start | bytes 86024 | tf_op jit(solution)/shard_map/ppermute | solution.py:494
  229.9 6.7 %collective-permute-start.26 = (f32[28,256]{1,0:T(8,128)S(1)}, f32[28,256]{1,0:T(8,128)S(1)}, u32[]{:S(2)}, u32[]{:S(2)}) collective-permute-start(f32[28,256]{1,0:T(8,128)S(1)} %add.93), channel_id=1, source_target_pairs={{0,128},{32,160},{64,192},{96,224},{128,0},{160,32},{192,64},{224,... | collective-permute-start | bytes 86024 | tf_op jit(solution)/shard_map/ppermute | solution.py:494
  236.5 10.1 %collective-permute-start.27 = (f32[28,256]{1,0:T(8,128)S(1)}, f32[28,256]{1,0:T(8,128)S(1)}, u32[]{:S(2)}, u32[]{:S(2)}) collective-permute-start(f32[28,256]{1,0:T(8,128)S(1)} %add.94), channel_id=1, source_target_pairs={{0,1},{1,0},{2,3},{3,2},{4,5},{5,4},{6,7},{7,6},{8,9},{9,8},{10,11... | collective-permute-start | bytes 86024 | tf_op jit(solution)/shard_map/ppermute | solution.py:29
  243.0 19.9 %all-to-all-start.3 = ((bf16[16,32,1024]{2,1,0:T(8,128)(2,1)}), bf16[16,32,1024]{2,1,0:T(8,128)(2,1)S(1)}, u32[]{:S(2)}, u32[]{:S(2)}) async-start(bf16[16,32,1024]{2,1,0:T(8,128)(2,1)} %bitcast.26), calls=%async_computation.3 | async-start | bytes 2097152 | tf_op jit(solution)/shard_map/all_to_all | solution.py:476
  (3 other events, 2.0 us)

commit v2 on v1

--- a/solution.py
+++ b/solution.py
@@ -214,52 +214,9 @@
     )
 
 
-def input_products(parts, others, slope, normed_in, normed, groups, rows):
+def input_pieces(parts, others, slope, normed_in, normed, w_own, out_rows, groups, rows, images):
     count = len(groups)
-    hidden = slope.shape[0]
-    held = rows * sum(len(group) for group in groups)
-    positions, feats = normed_in.shape
-
-    def kernel(*refs):
-        parts, others = refs[:count], refs[count : 2 * count]
-        slope_ref, in_ref, normed_ref, w_out, g_out, b_out, held_ref = refs[2 * count :]
-
-        @pl.when(pl.program_id(0) == 0)
-        def _():
-            preact_grads(parts, others, slope_ref, held_ref, groups, rows)
-            ones = jnp.ones((8, held), jnp.bfloat16)
-            b_out[...] = contract(ones, held_ref[...], 1, 1)
-
-        grads = held_ref[...]
-        w_out[...] = jnp.dot(
-            grads, of_groups(in_ref, groups, rows), preferred_element_type=jnp.float32
-        )
-        g_out[...] = jnp.dot(
-            grads, of_groups(normed_ref, groups, rows), preferred_element_type=jnp.float32
-        )
-
-    column = pl.BlockSpec((positions, TILE), lambda j: (0, j))
-    tile = pl.BlockSpec((hidden, TILE), lambda j: (0, j))
-    return pl.pallas_call(
-        kernel,
-        grid=(feats // TILE,),
-        in_specs=[whole(a.shape) for a in (*parts, *others)] + [whole(slope.shape), column, column],
-        out_specs=[tile, tile, whole((8, hidden))],
-        out_shape=[
-            jax.ShapeDtypeStruct((hidden, feats), jnp.float32),
-            jax.ShapeDtypeStruct((hidden, feats), jnp.float32),
-            jax.ShapeDtypeStruct((8, hidden), jnp.float32),
-        ],
-        scratch_shapes=[pltpu.VMEM((hidden, held), jnp.bfloat16)],
-        cost_estimate=pl.CostEstimate(
-            flops=4 * held * hidden * feats, bytes_accessed=8 * positions * feats, transcendentals=0
-        ),
-        name="input_products",
-    )(*parts, *others, slope, normed_in, normed)
-
-
-def input_pieces(part, other, slope, normed_in, normed, before, w_own, out_rows, rows, at, images):
-    hidden, held = part.shape
+    hidden, held = slope.shape
     own_feats = normed_in.shape[1]
     piece = own_feats // images
     width = hidden // 2
@@ -269,15 +226,17 @@
     total_rows = 2 * steps + b_rows + out_rows.shape[0]
     padded = -(-total_rows // 8) * 8
 
-    def kernel(part_ref, other_ref, slope_ref, in_ref, normed_ref, w_before, g_before, b_before,
-               w_ref, rows_ref, sent_ref, held_ref, vector_ref, column_ref):
+    def kernel(*refs):
+        parts, others = refs[:count], refs[count : 2 * count]
+        slope_ref, in_ref, normed_ref, w_ref, rows_ref = refs[2 * count : 2 * count + 5]
+        sent_ref, held_ref, vector_ref, column_ref = refs[2 * count + 5 :]
         step = pl.program_id(0)
 
         @pl.when(step == 0)
         def _():
-            preact_grads([part_ref], [other_ref], slope_ref, held_ref, [range(held // rows)], rows)
+            preact_grads(parts, others, slope_ref, held_ref, groups, rows)
             ones = jnp.ones((8, held), jnp.bfloat16)
-            sums = contract(ones, held_ref[...], 1, 1) + b_before[...]
+            sums = contract(ones, held_ref[...], 1, 1)
             vector_ref[...] = jnp.zeros_like(vector_ref)
             for i in range(b_rows):
                 vector_ref[2 * steps + i : 2 * steps + i + 1, :] = sums[
@@ -288,8 +247,12 @@
             column_ref[...] = jnp.broadcast_to(sums[0:1, :], (128, hidden)).T
 
         grads = held_ref[...]
-        w_grad = w_before[...] + jnp.dot(grads, in_ref[...], preferred_element_type=jnp.float32)
-        g_grad = g_before[...] + jnp.dot(grads, normed_ref[...], preferred_element_type=jnp.float32)
+        w_grad = jnp.dot(
+            grads, of_groups(in_ref, groups, rows), preferred_element_type=jnp.float32
+        )
+        g_grad = jnp.dot(
+            grads, of_groups(normed_ref, groups, rows), preferred_element_type=jnp.float32
+        )
         turned = w_grad.T.astype(jnp.bfloat16)
         for i in range(per_step):
             for half in range(2):
@@ -309,24 +272,14 @@
             for i in range(2 * images):
                 sent_ref[i, piece : piece + 2 * padded, :] = both
 
-    column = pl.BlockSpec((held, TILE), lambda j: (at, j))
+    column = pl.BlockSpec((held, TILE), lambda j: (0, j))
     tile = pl.BlockSpec((hidden, TILE), lambda j: (0, j))
     sent = (2 * images, piece + 2 * padded, width)
     return pl.pallas_call(
         kernel,
         grid=(steps,),
-        in_specs=[
-            whole(part.shape),
-            whole(part.shape),
-            pl.BlockSpec((hidden, held), lambda j: (0, at)),
-            column,
-            column,
-            tile,
-            tile,
-            whole((8, hidden)),
-            tile,
-            whole(out_rows.shape),
-        ],
+        in_specs=[whole(a.shape) for a in (*parts, *others)]
+        + [whole(slope.shape), column, column, tile, whole(out_rows.shape)],
         out_specs=whole(sent),
         scratch_shapes=[
             pltpu.VMEM((hidden, held), jnp.bfloat16),
@@ -338,7 +291,7 @@
             flops=4 * held * hidden * own_feats, bytes_accessed=8 * held * own_feats, transcendentals=0
         ),
         name="input_pieces",
-    )(part, other, slope, normed_in, normed, *before, w_own, out_rows)
+    )(*parts, *others, slope, normed_in, normed, w_own, out_rows)
 
 
 def split_terms(vector):
@@ -420,7 +373,7 @@
     def products(blocks):
         return hidden_products(weights, place, [low[i] for i in blocks], [high[i] for i in blocks])
 
-    groups = [(7, 1), (6, 2), (5, 3), (0,)]
+    groups = [(7, 1), (6, 2, 5, 3), (4,), (0,)]
     parts, others = [None] * 4, [None] * 4
     parts[3], rounded_own = products(groups[3])
     parts[3], rounded_own, seen_other = gate(parts[3], rounded_own, seen_other)
@@ -452,23 +405,22 @@
         low[5], low[3], hidden, others[0], others[3]
     )
     low[4] = along_z(low[5], 1)
+    high[5], high[3], hidden = gate(high[5], high[3], hidden)
+    high[4] = along_z(high[3], -1)
     parts[1], rounded = products(groups[1])
     others[1] = swap(rounded, "c")
-    high[5], high[3], parts[1] = gate(high[5], high[3], parts[1])
-    high[4] = along_z(high[3], -1)
+    low[4], hidden, parts[1] = gate(low[4], hidden, parts[1])
+    low_product = summed_product(hidden, low)
+    high[4], low_product = gate(high[4], low_product)
     parts[2], rounded = products(groups[2])
     others[2] = swap(rounded, "c")
-    low[4], hidden, parts[2], rounded = gate(low[4], hidden, parts[2], rounded)
-    low_product = summed_product(hidden, low)
-    low_product, normed_in, normed, slope = gate(low_product, normed_in, normed, slope)
+    low_product, normed_in, normed, slope, rounded = gate(
+        low_product, normed_in, normed, slope, rounded
+    )
     low_moved = lax.all_to_all(low_product, PLANE, 0, 0, tiled=True)
-    before = input_products(parts, others, slope, normed_in, normed, groups, rows)
-    high[4], *before = gate(high[4], *before)
-    part, rounded = products((4,))
-    other = swap(rounded, "c")
     high_product = summed_product(hidden, high)
     sent = input_pieces(
-        part, other, slope, normed_in, normed, before, w_own, out_part, rows, 4, img_count
+        parts, others, slope, normed_in, normed, w_own, out_part, groups, rows, img_count
     )
     sent, low_moved = gate(sent, low_moved)
     moved = lax.all_to_all(sent, PLANE, 0, 0, tiled=True)

time: 265 us -> 258 us (0.974)
  Pallas kernels: 61.9 us -> 56.6 us
    pallas_call x2 -> x1, Pallas kernels: 12.6 us -> 9.52 us  [input_pieces(): pl.pallas_call(kernel, grid=(steps,), in_specs=[whole(a.shape) for a in (...]
    pallas_call x5 -> x4, Pallas kernels: 21.1 us -> 18.7 us  [hidden_products(): pl.pallas_call(kernel, grid_spec=pltpu.PrefetchScalarGridSpec(num_scalar_...]
    ppermute x11 -> x10, starting transfers between devices: 18.5 us -> 19.4 us  [swap(): return lax.ppermute(array, axis, [(0, 1), (1, 0)])]
    ppermute x11 -> x10, waiting for transfers between devices: 24.5 us -> 24.2 us  [swap(): return lax.ppermute(array, axis, [(0, 1), (1, 0)])]
  transfers between devices with their start and end apart: 32 -> 31, of which waited for: 13 -> 13; matrix products, arithmetic and copies ran while one was open for 15% -> 15% of each run, Pallas kernels for 23% -> 22%
where the time goes in v2:
time: 258 us; the launch traced here: 257 us
  waiting for transfers between devices  94.2 us (37%)
  starting transfers between devices  58.3 us (23%)
  Pallas kernels  56.6 us (22%)
  local copies, waits for them, and re-layouts  29.8 us (12%)
  other arithmetic  15.4 us (6%)
    ppermute x10, waiting for transfers between devices, swap(): return lax.ppermute(array, axis, [(0, 1), (1, 0)])  24.2 us
    all_to_all x1, waiting for transfers between devices, one_step(): seen = lax.all_to_all(copies, 'z', 0, 0, tiled=True)  23.8 us
    ppermute x10, starting transfers between devices, swap(): return lax.ppermute(array, axis, [(0, 1), (1, 0)])  19.4 us
    pallas_call x4, Pallas kernels, hidden_products(): pl.pallas_call(kernel, grid_spec=pltpu.PrefetchScalarGridSpec(num_scalar_...  18.7 us
    pallas_call x1, Pallas kernels, forward(): pl.pallas_call(kernel, grid_spec=pltpu.PrefetchScalarGridSpec(num_scalar_...  16.4 us
    all_to_all x1, waiting for transfers between devices, one_step(): high_moved = lax.all_to_all(high_product, PLANE, 0, 0, tiled=True)  14.9 us
    ppermute x14, waiting for transfers between devices, along_z(): lax.ppermute(array, 'z', [(i, (i + shift) % count) for i in range(count)])  13.6 us
    pallas_call x2, Pallas kernels, summed_product(): pl.pallas_call(kernel, grid=(width // tile,), in_specs=[whole(left.shape)...  11.9 us
  transfers between devices with their start and end apart: 31, of which 13 were waited for; matrix products, arithmetic and copies ran while one was open for 15% of the time, Pallas kernels for 22%

profile of v2, /device:TPU:1, one launch (start us, length us, event | category | flops | bytes accessed | tf_op | source)
XLA Modules:
  0.0 257.4 jit_solution(9368120749696229795)
XLA Ops:
  0.6 2.2 broadcast_in_dim.67
  2.8 9.1 %all-to-all-start = ((bf16[8,72,1024]{2,1,0:T(8,128)(2,1)}), bf16[8,72,1024]{2,1,0:T(8,128)(2,1)S(1)}, u32[]{:S(2)}, u32[]{:S(2)}) async-start(bf16[8,72,1024]{2,1,0:T(8,128)(2,1)} %broadcast_in_dim.67), calls=%async_computation | async-start | bytes 2359296 | tf_op jit(solution)/shard_map/all_to_all | solution.py:319
  13.1 1.5 collective-permute-start.5
  14.5 1.2 collective-permute-start.6
  16.6 1.5 collective-permute-start.3
  18.1 1.2 collective-permute-start
  20.3 23.8 %all-to-all-done = bf16[8,72,1024]{2,1,0:T(8,128)(2,1)S(1)} async-done(((bf16[8,72,1024]{2,1,0:T(8,128)(2,1)}), bf16[8,72,1024]{2,1,0:T(8,128)(2,1)S(1)}, u32[]{:S(2)}, u32[]{:S(2)}) %all-to-all-start) | async-done | bytes 1179680 | tf_op jit(solution)/shard_map/all_to_all | solution.py:319
  44.0 1.2 collective-permute-start.11
  46.2 2.1 fusion.1
  49.2 3.5 %hidden_products.5 = (f32[512,256]{1,0:T(8,128)}, bf16[512,256]{1,0:T(8,128)(2,1)}) custom-call(s32[1]{0:T(128)} %bitcast.place_ref, bf16[256,2048]{1,0:T(8,128)(2,1)} %own_ref.7, bf16[256,2048]{1,0:T(8,128)(2,1)} %copy-done.1, bf16[256,1024]{1,0:T(8,128)(2,1)} %get-tuple-element.121.refs_0_, bf16[256,1024]{1,0:T(8,128)(2,1)} %get-tuple-element.120.refs_1_.refs_0_), custom_call_target="tpu_custom_call" | custom-call | flops 536870912 | bytes 1048576 | tf_op jit(solution)/shard_map/hidden_products/pallas_call | solution.py:93
  52.7 18.4 %collective-permute-done.11 = bf16[8,72,1024]{2,1,0:T(8,128)(2,1)} collective-permute-done((bf16[8,72,1024]{2,1,0:T(8,128)(2,1)S(1)}, bf16[8,72,1024]{2,1,0:T(8,128)(2,1)}, u32[]{:S(2)}, u32[]{:S(2)}) %collective-permute-start.11) | collective-permute-done | bytes 1179680 | tf_op jit(solution)/shard_map/ppermute | solution.py:29
  71.1 3.0 %fusion.19 = (bf16[8,1,2,72,1024]{4,3,2,1,0:T(8,128)(2,1)S(1)}, bf16[8,2,72,1024]{3,2,1,0:T(8,128)(2,1)}) fusion(bf16[8,1,72,1024]{3,2,1,0:T(8,128)(2,1)} %bitcast.18, bf16[8,1,72,1024]{3,2,1,0:T(8,128)(2,1)S(1)} %bitcast.48), kind=kLoop, calls=%fused_computation.71 | loop fusion | flops 1179648 | bytes 7077888 | tf_op jit(solution)/shard_map/stack | solution.py:387
  74.1 1.5 collective-permute-start.12
  82.3 1.3 copy.77
  88.6 1.5 collective-permute-start.16
  90.1 4.7 %collective-permute-done.4 = bf16[1032,256]{1,0:T(8,128)(2,1)S(1)} collective-permute-done((bf16[1032,256]{1,0:T(8,128)(2,1)}, bf16[1032,256]{1,0:T(8,128)(2,1)S(1)}, u32[]{:S(2)}, u32[]{:S(2)}) %collective-permute-start.4) | collective-permute-done | bytes 528416 | tf_op jit(solution)/shard_map/ppermute | solution.py:29
  99.0 2.3 copy.58
  101.4 1.9 constant_dynamic-slice_fusion
  103.2 2.0 copy.59
  105.4 1.5 collective-permute-start.7
  106.9 1.2 collective-permute-start.8
  108.1 4.7 %hidden_products.4 = (f32[512,512]{1,0:T(8,128)}, bf16[512,512]{1,0:T(8,128)(2,1)}) custom-call(s32[1]{0:T(128)} %bitcast.place_ref, bf16[256,2048]{1,0:T(8,128)(2,1)} %own_ref.7, bf16[256,2048]{1,0:T(8,128)(2,1)} %copy-done.1, bf16[256,1024]{1,0:T(8,128)(2,1)} %collective-permute-done.1.refs_0_.refs_7_, bf16[256,1024]{1,0:T(8,128)(2,1)} %collective-permute-done.2.refs_1_, ...), custom_call_target="tpu_custom_call" | custom-call | flops 1073741824 | bytes 2097152 | tf_op jit(solution)/shard_map/hidden_products/pallas_call | solution.py:93
  112.8 1.3 collective-permute-start.13
  115.5 4.2 %collective-permute-done.7.refs_0_.refs_6_ = bf16[256,1024]{1,0:T(8,128)(2,1)} collective-permute-done((bf16[256,1024]{1,0:T(8,128)(2,1)}, bf16[256,1024]{1,0:T(8,128)(2,1)}, u32[]{:S(2)}, u32[]{:S(2)}) %collective-permute-start.7) | collective-permute-done | bytes 524320 | tf_op jit(solution)/shard_map/ppermute | solution.py:39
  119.7 4.9 %collective-permute-done.8.refs_1_.refs_2_ = bf16[256,1024]{1,0:T(8,128)(2,1)} collective-permute-done((bf16[256,1024]{1,0:T(8,128)(2,1)}, bf16[256,1024]{1,0:T(8,128)(2,1)}, u32[]{:S(2)}, u32[]{:S(2)}) %collective-permute-start.8) | collective-permute-done | bytes 524320 | tf_op jit(solution)/shard_map/ppermute | solution.py:39
  124.6 1.5 collective-permute-start.10
  126.1 4.3 %pad_maximum_fusion = bf16[8,2,2,72,1024]{4,3,2,1,0:T(8,128)(2,1)} fusion(bf16[8,1,2,72,1024]{4,3,2,1,0:T(8,128)(2,1)} %bitcast.21, bf16[8,1,2,72,1024]{4,3,2,1,0:T(8,128)(2,1)S(1)} %get-tuple-element.116), kind=kLoop, calls=%fused_computation | loop fusion | flops 2359296 | bytes 9437184 | tf_op jit(solution)/shard_map/stack | solution.py:387
  130.4 2.5 collective-permute-start.14
  132.9 16.4 %forward.1 = (bf16[2048,512]{1,0:T(8,128)(2,1)}, bf16[2048,512]{1,0:T(8,128)(2,1)}, bf16[512,2048]{1,0:T(8,128)(2,1)}, f32[512,2048]{1,0:T(8,128)}) custom-call(s32[8]{0:T(128)} %copy-done.16, s32[8]{0:T(128)} %fusion.17.window_ref, s32[4]{0:T(128)} %copy-done.15, s32[1]{0:T(128)} %bitcast.14.core_ref, bf16[8,288,1024]{2,1,0:T(8,128)(2,1)} %bitcast.49, ...), custom_call_target="tpu_custom_call" | custom-call | flops 4563402752 | bytes 20971520 | tf_op jit(solution)/shard_map/forward/pallas_call | solution.py:160
  149.4 2.7 %collective-permute-start.20 = (bf16[256,1024]{1,0:T(8,128)(2,1)}, bf16[256,1024]{1,0:T(8,128)(2,1)S(1)}, u32[]{:S(2)}, u32[]{:S(2)}) collective-permute-start(bf16[256,1024]{1,0:T(8,128)(2,1)} %collective-permute-done.19.refs_7_.refs_3_), channel_id=1, source_target_pairs={{0,224},{32,0},{64,32},{96,64},{128,96},{160,128},{192,160},{224,1... | collective-permute-start | bytes 1572872 | tf_op jit(solution)/shard_map/ppermute | solution.py:39
  152.1 7.1 %hidden_products.6 = (f32[512,1024]{1,0:T(8,128)}, bf16[512,1024]{1,0:T(8,128)(2,1)}) custom-call(s32[1]{0:T(128)} %bitcast.place_ref, bf16[256,2048]{1,0:T(8,128)(2,1)} %own_ref.7, bf16[256,2048]{1,0:T(8,128)(2,1)} %copy-done.1, bf16[256,1024]{1,0:T(8,128)(2,1)} %collective-permute-done.7.refs_0_.refs_6_, ...), custom_call_target="tpu_custom_call" | custom-call | flops 2147483648 | bytes 4194304 | tf_op jit(solution)/shard_map/hidden_products/pallas_call | solution.py:93
  159.8 4.5 %collective-permute-done.15.refs_4_.refs_0_ = bf16[256,1024]{1,0:T(8,128)(2,1)S(1)} collective-permute-done((bf16[256,1024]{1,0:T(8,128)(2,1)}, bf16[256,1024]{1,0:T(8,128)(2,1)S(1)}, u32[]{:S(2)}, u32[]{:S(2)}) %collective-permute-start.15) | collective-permute-done | bytes 524320 | tf_op jit(solution)/shard_map/ppermute | solution.py:39
  165.1 5.9 %summed_product.2 = bf16[512,1024]{1,0:T(8,128)(2,1)} custom-call(bf16[512,2048]{1,0:T(8,128)(2,1)} %get-tuple-element.92.left_ref, bf16[256,1024]{1,0:T(8,128)(2,1)} %get-tuple-element.121.refs_0_, bf16[256,1024]{1,0:T(8,128)(2,1)} %collective-permute-done.2.refs_1_, bf16[256,1024]{1,0:T(8,128)(2,1)} %collective-permute-done.8.refs_1_.refs_2_, ...), custom_call_target="tpu_custom_call" | custom-call | flops 2147483648 | bytes 10485760 | tf_op jit(solution)/shard_map/summed_product/pallas_call | solution.py:60
  171.8 3.5 %hidden_products.7 = (f32[512,256]{1,0:T(8,128)}, bf16[512,256]{1,0:T(8,128)(2,1)}) custom-call(s32[1]{0:T(128)} %bitcast.place_ref, bf16[256,2048]{1,0:T(8,128)(2,1)} %own_ref.7, bf16[256,2048]{1,0:T(8,128)(2,1)} %copy-done.1, bf16[256,1024]{1,0:T(8,128)(2,1)} %copy-done.8, bf16[256,1024]{1,0:T(8,128)(2,1)} %copy-done.7), custom_call_target="tpu_custom_call" | custom-call | flops 536870912 | bytes 1048576 | tf_op jit(solution)/shard_map/hidden_products/pallas_call | solution.py:93
  175.3 6.6 %all-to-all-start.1 = ((bf16[16,32,1024]{2,1,0:T(8,128)(2,1)}), bf16[16,32,1024]{2,1,0:T(8,128)(2,1)S(1)}, u32[]{:S(2)}, u32[]{:S(2)}) async-start(bf16[16,32,1024]{2,1,0:T(8,128)(2,1)} %bitcast.23), calls=%async_computation.1 | async-start | bytes 2097152 | tf_op jit(solution)/shard_map/all_to_all | solution.py:420
  181.9 1.2 collective-permute-start.22
  185.4 9.5 %input_pieces.1 = bf16[16,96,256]{2,1,0:T(8,128)(2,1)} custom-call(f32[512,512]{1,0:T(8,128)} %get-tuple-element.64.refs_0_, f32[512,1024]{1,0:T(8,128)} %get-tuple-element.90.refs_1_, f32[512,256]{1,0:T(8,128)} %get-tuple-element.94.refs_2_, f32[512,256]{1,0:T(8,128)} %get-tuple-element.95.refs_3_, bf16[512,512]{1,0:T(8,128)(2,1)} %copy-done.6, ...), custom_call_target="tpu_custom_call" | custom-call | flops 2147483648 | bytes 8388608 | tf_op jit(solution)/shard_map/input_pieces/pallas_call | solution.py:278
  194.9 1.5 all-to-all-done.1
  196.4 5.5 %all-to-all-start.2 = ((bf16[16,96,256]{2,1,0:T(8,128)(2,1)}), bf16[16,96,256]{2,1,0:T(8,128)(2,1)S(1)}, u32[]{:S(2)}, u32[]{:S(2)}) async-start(bf16[16,96,256]{2,1,0:T(8,128)(2,1)} %input_pieces.1), calls=%async_computation.2 | async-start | bytes 1572864 | tf_op jit(solution)/shard_map/all_to_all | solution.py:426
  202.1 6.0 %summed_product.3 = bf16[512,1024]{1,0:T(8,128)(2,1)} custom-call(bf16[512,2048]{1,0:T(8,128)(2,1)} %get-tuple-element.92.left_ref, bf16[256,1024]{1,0:T(8,128)(2,1)} %get-tuple-element.120.refs_1_.refs_0_, bf16[256,1024]{1,0:T(8,128)(2,1)} %collective-permute-done.6.refs_3_.refs_1_, bf16[256,1024]{1,0:T(8,128)(2,1)} %collective-permute-done.17.refs_5_.refs_2_, ...), custom_call_target="tpu_custom_call" | custom-call | flops 2147483648 | bytes 10485760 | tf_op jit(solution)/shard_map/summed_product/pallas_call | solution.py:60
  208.1 5.2 %all-to-all-done.2 = bf16[16,96,256]{2,1,0:T(8,128)(2,1)S(1)} async-done(((bf16[16,96,256]{2,1,0:T(8,128)(2,1)}), bf16[16,96,256]{2,1,0:T(8,128)(2,1)S(1)}, u32[]{:S(2)}, u32[]{:S(2)}) %all-to-all-start.2) | async-done | bytes 786464 | tf_op jit(solution)/shard_map/all_to_all | solution.py:426
  213.6 2.8 %collective-permute-done.23 = f32[28,256]{1,0:T(8,128)S(1)} collective-permute-done((f32[28,256]{1,0:T(8,128)S(1)}, f32[28,256]{1,0:T(8,128)S(1)}, u32[]{:S(2)}, u32[]{:S(2)}) %collective-permute-start.23) | collective-permute-done | bytes 28704 | tf_op jit(solution)/shard_map/ppermute | solution.py:446
  216.5 3.8 %collective-permute-done.24 = f32[28,256]{1,0:T(8,128)S(1)} collective-permute-done((f32[28,256]{1,0:T(8,128)S(1)}, f32[28,256]{1,0:T(8,128)S(1)}, u32[]{:S(2)}, u32[]{:S(2)}) %collective-permute-start.24) | collective-permute-done | bytes 28704 | tf_op jit(solution)/shard_map/ppermute | solution.py:446
  220.3 2.2 collective-permute-start.25
  222.6 4.4 %collective-permute-done.25 = f32[28,256]{1,0:T(8,128)S(1)} collective-permute-done((f32[28,256]{1,0:T(8,128)S(1)}, f32[28,256]{1,0:T(8,128)S(1)}, u32[]{:S(2)}, u32[]{:S(2)}) %collective-permute-start.25) | collective-permute-done | bytes 28704 | tf_op jit(solution)/shard_map/ppermute | solution.py:446
  227.0 7.1 %collective-permute-start.26 = (f32[28,256]{1,0:T(8,128)S(1)}, f32[28,256]{1,0:T(8,128)S(1)}, u32[]{:S(2)}, u32[]{:S(2)}) collective-permute-start(f32[28,256]{1,0:T(8,128)S(1)} %add.94), channel_id=1, source_target_pairs={{0,1},{1,0},{2,3},{3,2},{4,5},{5,4},{6,7},{7,6},{8,9},{9,8},{10,11... | collective-permute-start | bytes 86024 | tf_op jit(solution)/shard_map/ppermute | solution.py:29
  234.9 3.7 %all-to-all-start.3 = ((bf16[16,32,1024]{2,1,0:T(8,128)(2,1)}), bf16[16,32,1024]{2,1,0:T(8,128)(2,1)S(1)}, u32[]{:S(2)}, u32[]{:S(2)}) async-start(bf16[16,32,1024]{2,1,0:T(8,128)(2,1)} %bitcast.26), calls=%async_computation.3 | async-start | bytes 2097152 | tf_op jit(solution)/shard_map/all_to_all | solution.py:428
  241.6 14.9 %all-to-all-done.3 = bf16[16,32,1024]{2,1,0:T(8,128)(2,1)S(1)} async-done(((bf16[16,32,1024]{2,1,0:T(8,128)(2,1)}), bf16[16,32,1024]{2,1,0:T(8,128)(2,1)S(1)}, u32[]{:S(2)}, u32[]{:S(2)}) %all-to-all-start.3) | async-done | bytes 1048608 | tf_op jit(solution)/shard_map/all_to_all | solution.py:428
  (143 shorter events, 32.0 us)
Async XLA Ops:
  0.6 11.4 %copy-start.4 = (bf16[1,256,2048]{2,1,0:T(8,128)(2,1)S(1)}, bf16[1,256,2048]{2,1,0:T(8,128)(2,1)}, u32[]{:S(2)}) copy-start(bf16[1,256,2048]{2,1,0:T(8,128)(2,1)} %param.15) | copy-start | bytes 3145732
  2.8 12.9 %copy-start.11 = (bf16[512,256]{1,0:T(8,128)(2,1)S(1)}, bf16[512,256]{1,0:T(8,128)(2,1)}, u32[]{:S(2)}) copy-start(bf16[512,256]{1,0:T(8,128)(2,1)} %param.12) | copy-start | bytes 786436
  2.8 15.3 %copy-start = (bf16[256,2048]{1,0:T(8,128)(2,1)S(1)}, bf16[256,2048]{1,0:T(8,128)(2,1)}, u32[]{:S(2)}) copy-start(bf16[256,2048]{1,0:T(8,128)(2,1)} %own_ref.7) | copy-start | bytes 3145732
  2.8 16.5 %copy-start.12 = (s32[1,2304]{1,0:T(1,128)S(1)}, s32[1,2304]{1,0:T(1,128)}, u32[]{:S(2)}) copy-start(s32[1,2304]{1,0:T(1,128)} %param.17) | copy-start | bytes 27652
  2.8 16.5 %copy-start.13 = (s32[1,2]{1,0:T(1,128)S(1)}, s32[1,2]{1,0:T(1,128)}, u32[]{:S(2)}) copy-start(s32[1,2]{1,0:T(1,128)} %param.16) | copy-start | bytes 28
  2.8 41.2 %all-to-all-start = ((bf16[8,72,1024]{2,1,0:T(8,128)(2,1)}), bf16[8,72,1024]{2,1,0:T(8,128)(2,1)S(1)}, u32[]{:S(2)}, u32[]{:S(2)}) async-start(bf16[8,72,1024]{2,1,0:T(8,128)(2,1)} %broadcast_in_dim.67), calls=%async_computation | async-start | bytes 2359296 | tf_op jit(solution)/shard_map/all_to_all | solution.py:319
  13.1 75.5 %collective-permute-start.5 = (bf16[256,1024]{1,0:T(8,128)(2,1)}, bf16[256,1024]{1,0:T(8,128)(2,1)}, u32[]{:S(2)}, u32[]{:S(2)}) collective-permute-start(bf16[256,1024]{1,0:T(8,128)(2,1)} %get-tuple-element.120.refs_1_.refs_0_), channel_id=1, source_target_pairs={{0,32},{32,64},{64,96},{96,128},{128,160},{160,192},{192,224},{224... | collective-permute-start | bytes 1572872 | tf_op jit(solution)/shard_map/ppermute | solution.py:39
  14.5 74.1 %collective-permute-start.6 = (bf16[256,1024]{1,0:T(8,128)(2,1)}, bf16[256,1024]{1,0:T(8,128)(2,1)}, u32[]{:S(2)}, u32[]{:S(2)}) collective-permute-start(bf16[256,1024]{1,0:T(8,128)(2,1)} %get-tuple-element.120.refs_1_.refs_0_), channel_id=1, source_target_pairs={{0,224},{32,0},{64,32},{96,64},{128,96},{160,128},{192,160},{224,1... | collective-permute-start | bytes 1572872 | tf_op jit(solution)/shard_map/ppermute | solution.py:39
  16.6 60.5 %collective-permute-start.3 = (bf16[512,256]{0,1:T(8,128)(2,1)}, bf16[512,256]{0,1:T(8,128)(2,1)}, u32[]{:S(2)}, u32[]{:S(2)}) collective-permute-start(bf16[512,256]{0,1:T(8,128)(2,1)} %copy.50), channel_id=1, source_target_pairs={{0,1},{1,0},{2,3},{3,2},{4,5},{5,4},{6,7},{7,6},{8,9},{9,8},{10,11... | collective-permute-start | bytes 786440 | tf_op jit(solution)/shard_map/ppermute | solution.py:29
  18.1 30.1 %collective-permute-start = (bf16[256,2048]{1,0:T(8,128)(2,1)S(1)}, bf16[256,2048]{1,0:T(8,128)(2,1)S(1)}, u32[]{:S(2)}, u32[]{:S(2)}) collective-permute-start(bf16[256,2048]{1,0:T(8,128)(2,1)S(1)} %copy-done), channel_id=1, source_target_pairs={{0,16},{16,0},{1,17},{17,1},{2,18},{18,2},{3,19},{19,3},{4,20},{20... | collective-permute-start | bytes 3145736 | tf_op jit(solution)/shard_map/ppermute | solution.py:29
  20.1 25.2 %copy-start.16 = (s32[8]{0:T(128)}, s32[8]{0:T(128)S(1)}, u32[]{:S(2)}) copy-start(s32[8]{0:T(128)S(1)} %fusion.16.base_ref) | copy-start | bytes 100
  44.0 27.0 %collective-permute-start.11 = (bf16[8,72,1024]{2,1,0:T(8,128)(2,1)S(1)}, bf16[8,72,1024]{2,1,0:T(8,128)(2,1)}, u32[]{:S(2)}, u32[]{:S(2)}) collective-permute-start(bf16[8,72,1024]{2,1,0:T(8,128)(2,1)S(1)} %all-to-all-done), channel_id=1, source_target_pairs={{0,16},{16,0},{1,17},{17,1},{2,18},{18,2},{3,19},{19,3},{4,20},{20... | collective-permute-start | bytes 3538952 | tf_op jit(solution)/shard_map/ppermute | solution.py:29
  48.2 1.0 copy-start.1
  48.2 57.1 %collective-permute-start.1 = (bf16[256,1024]{1,0:T(8,128)(2,1)}, bf16[256,1024]{1,0:T(8,128)(2,1)}, u32[]{:S(2)}, u32[]{:S(2)}) collective-permute-start(bf16[256,1024]{1,0:T(8,128)(2,1)} %get-tuple-element.121.refs_0_), channel_id=1, source_target_pairs={{0,32},{32,64},{64,96},{96,128},{128,160},{160,192},{192,224},{224... | collective-permute-start | bytes 1572872 | tf_op jit(solution)/shard_map/ppermute | solution.py:39
  71.1 4.5 %copy-start.14 = (f32[256]{0:T(256)S(1)}, f32[256]{0:T(256)}, u32[]{:S(2)}) copy-start(f32[256]{0:T(256)} %param.13) | copy-start | bytes 3076
  74.1 52.0 %collective-permute-start.12 = (bf16[8,2,72,1024]{3,2,1,0:T(8,128)(2,1)}, bf16[8,2,72,1024]{3,2,1,0:T(8,128)(2,1)}, u32[]{:S(2)}, u32[]{:S(2)}) collective-permute-start(bf16[8,2,72,1024]{3,2,1,0:T(8,128)(2,1)} %get-tuple-element.117), channel_id=1, source_target_pairs={{0,1},{1,0},{2,3},{3,2},{4,5},{5,4},{6,7},{7,6},{8,9},{9,8},{10,11... | collective-permute-start | bytes 7077896 | tf_op jit(solution)/shard_map/ppermute | solution.py:29
  80.9 13.9 %collective-permute-start.4 = (bf16[1032,256]{1,0:T(8,128)(2,1)}, bf16[1032,256]{1,0:T(8,128)(2,1)S(1)}, u32[]{:S(2)}, u32[]{:S(2)}) collective-permute-start(bf16[1032,256]{1,0:T(8,128)(2,1)} %copy.55), channel_id=1, source_target_pairs={{0,16},{16,0},{1,17},{17,1},{2,18},{18,2},{3,19},{19,3},{4,20},{20... | collective-permute-start | bytes 1585160 | tf_op jit(solution)/shard_map/ppermute | solution.py:29
  88.6 16.8 %collective-permute-start.2 = (bf16[256,1024]{1,0:T(8,128)(2,1)}, bf16[256,1024]{1,0:T(8,128)(2,1)}, u32[]{:S(2)}, u32[]{:S(2)}) collective-permute-start(bf16[256,1024]{1,0:T(8,128)(2,1)} %get-tuple-element.121.refs_0_), channel_id=1, source_target_pairs={{0,224},{32,0},{64,32},{96,64},{128,96},{160,128},{192,160},{224,1... | collective-permute-start | bytes 1572872 | tf_op jit(solution)/shard_map/ppermute | solution.py:39
  88.6 24.2 %collective-permute-start.16 = (bf16[256,1024]{1,0:T(8,128)(2,1)}, bf16[256,1024]{1,0:T(8,128)(2,1)}, u32[]{:S(2)}, u32[]{:S(2)}) collective-permute-start(bf16[256,1024]{1,0:T(8,128)(2,1)} %collective-permute-done.5.refs_2_.refs_7_), channel_id=1, source_target_pairs={{0,32},{32,64},{64,96},{96,128},{128,160},{160,192},{192,224},{224... | collective-permute-start | bytes 1572872 | tf_op jit(solution)/shard_map/ppermute | solution.py:39
  94.8 20.2 %collective-permute-start.17 = (bf16[256,1024]{1,0:T(8,128)(2,1)}, bf16[256,1024]{1,0:T(8,128)(2,1)}, u32[]{:S(2)}, u32[]{:S(2)}) collective-permute-start(bf16[256,1024]{1,0:T(8,128)(2,1)} %collective-permute-done.6.refs_3_.refs_1_), channel_id=1, source_target_pairs={{0,224},{32,0},{64,32},{96,64},{128,96},{160,128},{192,160},{224,1... | collective-permute-start | bytes 1572872 | tf_op jit(solution)/shard_map/ppermute | solution.py:39
  97.0 0.8 copy-start.2
  99.0 6.2 %copy-start.3 = (bf16[1032,256]{0,1:T(8,128)(2,1)S(1)}, bf16[1032,256]{0,1:T(8,128)(2,1)}, u32[]{:S(2)}) copy-start(bf16[1032,256]{0,1:T(8,128)(2,1)} %copy-done.2) | copy-start | bytes 1585156
  105.4 14.3 %collective-permute-start.7 = (bf16[256,1024]{1,0:T(8,128)(2,1)}, bf16[256,1024]{1,0:T(8,128)(2,1)}, u32[]{:S(2)}, u32[]{:S(2)}) collective-permute-start(bf16[256,1024]{1,0:T(8,128)(2,1)} %collective-permute-done.1.refs_0_.refs_7_), channel_id=1, source_target_pairs={{0,32},{32,64},{64,96},{96,128},{128,160},{160,192},{192,224},{224... | collective-permute-start | bytes 1572872 | tf_op jit(solution)/shard_map/ppermute | solution.py:39
  106.9 17.7 %collective-permute-start.8 = (bf16[256,1024]{1,0:T(8,128)(2,1)}, bf16[256,1024]{1,0:T(8,128)(2,1)}, u32[]{:S(2)}, u32[]{:S(2)}) collective-permute-start(bf16[256,1024]{1,0:T(8,128)(2,1)} %collective-permute-done.2.refs_1_), channel_id=1, source_target_pairs={{0,224},{32,0},{64,32},{96,64},{128,96},{160,128},{192,160},{224,1... | collective-permute-start | bytes 1572872 | tf_op jit(solution)/shard_map/ppermute | solution.py:39
  112.8 17.6 %collective-permute-start.13 = (bf16[512,512]{1,0:T(8,128)(2,1)}, bf16[512,512]{1,0:T(8,128)(2,1)S(1)}, u32[]{:S(2)}, u32[]{:S(2)}) collective-permute-start(bf16[512,512]{1,0:T(8,128)(2,1)} %get-tuple-element.79), channel_id=1, source_target_pairs={{0,1},{1,0},{2,3},{3,2},{4,5},{5,4},{6,7},{7,6},{8,9},{9,8},{10,11... | collective-permute-start | bytes 1572872 | tf_op jit(solution)/shard_map/ppermute | solution.py:29
  115.0 34.4 %collective-permute-start.18 = (bf16[256,1024]{1,0:T(8,128)(2,1)}, bf16[256,1024]{1,0:T(8,128)(2,1)}, u32[]{:S(2)}, u32[]{:S(2)}) collective-permute-start(bf16[256,1024]{1,0:T(8,128)(2,1)} %collective-permute-done.16.refs_4_.refs_6_), channel_id=1, source_target_pairs={{0,32},{32,64},{64,96},{96,128},{128,160},{160,192},{192,224},{224... | collective-permute-start | bytes 1572872 | tf_op jit(solution)/shard_map/ppermute | solution.py:39
  119.7 29.7 %collective-permute-start.19 = (bf16[256,1024]{1,0:T(8,128)(2,1)}, bf16[256,1024]{1,0:T(8,128)(2,1)}, u32[]{:S(2)}, u32[]{:S(2)}) collective-permute-start(bf16[256,1024]{1,0:T(8,128)(2,1)} %collective-permute-done.17.refs_5_.refs_2_), channel_id=1, source_target_pairs={{0,224},{32,0},{64,32},{96,64},{128,96},{160,128},{192,160},{224,1... | collective-permute-start | bytes 1572872 | tf_op jit(solution)/shard_map/ppermute | solution.py:39
  124.6 24.7 %collective-permute-start.10 = (bf16[256,1024]{1,0:T(8,128)(2,1)}, bf16[256,1024]{1,0:T(8,128)(2,1)}, u32[]{:S(2)}, u32[]{:S(2)}) collective-permute-start(bf16[256,1024]{1,0:T(8,128)(2,1)} %collective-permute-done.8.refs_1_.refs_2_), channel_id=1, source_target_pairs={{0,224},{32,0},{64,32},{96,64},{128,96},{160,128},{192,160},{224,1... | collective-permute-start | bytes 1572872 | tf_op jit(solution)/shard_map/ppermute | solution.py:39
  126.1 23.2 %collective-permute-start.9 = (bf16[256,1024]{1,0:T(8,128)(2,1)}, bf16[256,1024]{1,0:T(8,128)(2,1)}, u32[]{:S(2)}, u32[]{:S(2)}) collective-permute-start(bf16[256,1024]{1,0:T(8,128)(2,1)} %collective-permute-done.7.refs_0_.refs_6_), channel_id=1, source_target_pairs={{0,32},{32,64},{64,96},{96,128},{128,160},{160,192},{192,224},{224... | collective-permute-start | bytes 1572872 | tf_op jit(solution)/shard_map/ppermute | solution.py:39
  126.1 4.3 %copy-start.17 = (bf16[512,256]{1,0:T(8,128)(2,1)S(1)}, bf16[512,256]{1,0:T(8,128)(2,1)}, u32[]{:S(2)}) copy-start(bf16[512,256]{1,0:T(8,128)(2,1)} %get-tuple-element.80) | copy-start | bytes 786436
  130.4 18.9 %copy-start.6 = (bf16[512,512]{1,0:T(8,128)(2,1)}, bf16[512,512]{1,0:T(8,128)(2,1)S(1)}, u32[]{:S(2)}) copy-start(bf16[512,512]{1,0:T(8,128)(2,1)S(1)} %collective-permute-done.13.refs_4_) | copy-start | bytes 1572868
  130.4 18.9 %collective-permute-start.14 = (bf16[512,256]{1,0:T(8,128)(2,1)S(1)}, bf16[512,256]{1,0:T(8,128)(2,1)S(1)}, u32[]{:S(2)}, u32[]{:S(2)}) collective-permute-start(bf16[512,256]{1,0:T(8,128)(2,1)S(1)} %copy-done.17), channel_id=1, source_target_pairs={{0,1},{1,0},{2,3},{3,2},{4,5},{5,4},{6,7},{7,6},{8,9},{9,8},{10,11... | collective-permute-start | bytes 786440 | tf_op jit(solution)/shard_map/ppermute | solution.py:29
  149.3 9.9 %copy-start.9 = (bf16[512,256]{1,0:T(8,128)(2,1)}, bf16[512,256]{1,0:T(8,128)(2,1)S(1)}, u32[]{:S(2)}) copy-start(bf16[512,256]{1,0:T(8,128)(2,1)S(1)} %collective-permute-done.14.refs_7_) | copy-start | bytes 786436
  149.3 15.0 %collective-permute-start.15 = (bf16[256,1024]{1,0:T(8,128)(2,1)}, bf16[256,1024]{1,0:T(8,128)(2,1)S(1)}, u32[]{:S(2)}, u32[]{:S(2)}) collective-permute-start(bf16[256,1024]{1,0:T(8,128)(2,1)} %collective-permute-done.9.refs_2_.refs_5_), channel_id=1, source_target_pairs={{0,32},{32,64},{64,96},{96,128},{128,160},{160,192},{192,224},{224... | collective-permute-start | bytes 1572872 | tf_op jit(solution)/shard_map/ppermute | solution.py:39
  149.4 21.6 %collective-permute-start.20 = (bf16[256,1024]{1,0:T(8,128)(2,1)}, bf16[256,1024]{1,0:T(8,128)(2,1)S(1)}, u32[]{:S(2)}, u32[]{:S(2)}) collective-permute-start(bf16[256,1024]{1,0:T(8,128)(2,1)} %collective-permute-done.19.refs_7_.refs_3_), channel_id=1, source_target_pairs={{0,224},{32,0},{64,32},{96,64},{128,96},{160,128},{192,160},{224,1... | collective-permute-start | bytes 1572872 | tf_op jit(solution)/shard_map/ppermute | solution.py:39
  159.2 25.1 %collective-permute-start.21 = (bf16[512,1024]{1,0:T(8,128)(2,1)}, bf16[512,1024]{1,0:T(8,128)(2,1)S(1)}, u32[]{:S(2)}, u32[]{:S(2)}) collective-permute-start(bf16[512,1024]{1,0:T(8,128)(2,1)} %get-tuple-element.97), channel_id=1, source_target_pairs={{0,1},{1,0},{2,3},{3,2},{4,5},{5,4},{6,7},{7,6},{8,9},{9,8},{10,11... | collective-permute-start | bytes 3145736 | tf_op jit(solution)/shard_map/ppermute | solution.py:29
  164.3 0.8 copy-start.8
  171.1 0.8 copy-start.7
  175.3 6.6 %copy-start.18 = (bf16[512,256]{1,0:T(8,128)(2,1)S(1)}, bf16[512,256]{1,0:T(8,128)(2,1)}, u32[]{:S(2)}) copy-start(bf16[512,256]{1,0:T(8,128)(2,1)} %get-tuple-element.98) | copy-start | bytes 786436
  175.3 21.1 %all-to-all-start.1 = ((bf16[16,32,1024]{2,1,0:T(8,128)(2,1)}), bf16[16,32,1024]{2,1,0:T(8,128)(2,1)S(1)}, u32[]{:S(2)}, u32[]{:S(2)}) async-start(bf16[16,32,1024]{2,1,0:T(8,128)(2,1)} %bitcast.23), calls=%async_computation.1 | async-start | bytes 2097152 | tf_op jit(solution)/shard_map/all_to_all | solution.py:420
  181.9 2.4 collective-permute-start.22
  184.3 1.1 copy-start.5
  196.4 16.8 %all-to-all-start.2 = ((bf16[16,96,256]{2,1,0:T(8,128)(2,1)}), bf16[16,96,256]{2,1,0:T(8,128)(2,1)S(1)}, u32[]{:S(2)}, u32[]{:S(2)}) async-start(bf16[16,96,256]{2,1,0:T(8,128)(2,1)} %input_pieces.1), calls=%async_computation.2 | async-start | bytes 1572864 | tf_op jit(solution)/shard_map/all_to_all | solution.py:426
  213.5 2.9 %collective-permute-start.23 = (f32[28,256]{1,0:T(8,128)S(1)}, f32[28,256]{1,0:T(8,128)S(1)}, u32[]{:S(2)}, u32[]{:S(2)}) collective-permute-start(f32[28,256]{1,0:T(8,128)S(1)} %pad_maximum_fusion.4), channel_id=1, source_target_pairs={{0,32},{32,0},{64,96},{96,64},{128,160},{160,128},{192,224},{224,1... | collective-permute-start | bytes 86024 | tf_op jit(solution)/shard_map/ppermute | solution.py:446
  216.4 3.9 %collective-permute-start.24 = (f32[28,256]{1,0:T(8,128)S(1)}, f32[28,256]{1,0:T(8,128)S(1)}, u32[]{:S(2)}, u32[]{:S(2)}) collective-permute-start(f32[28,256]{1,0:T(8,128)S(1)} %fusion.18), channel_id=1, source_target_pairs={{0,64},{32,96},{64,0},{96,32},{128,192},{160,224},{192,128},{224,1... | collective-permute-start | bytes 86024 | tf_op jit(solution)/shard_map/ppermute | solution.py:446
  220.3 6.7 %collective-permute-start.25 = (f32[28,256]{1,0:T(8,128)S(1)}, f32[28,256]{1,0:T(8,128)S(1)}, u32[]{:S(2)}, u32[]{:S(2)}) collective-permute-start(f32[28,256]{1,0:T(8,128)S(1)} %add.93), channel_id=1, source_target_pairs={{0,128},{32,160},{64,192},{96,224},{128,0},{160,32},{192,64},{224,... | collective-permute-start | bytes 86024 | tf_op jit(solution)/shard_map/ppermute | solution.py:446
  227.0 11.6 %collective-permute-start.26 = (f32[28,256]{1,0:T(8,128)S(1)}, f32[28,256]{1,0:T(8,128)S(1)}, u32[]{:S(2)}, u32[]{:S(2)}) collective-permute-start(f32[28,256]{1,0:T(8,128)S(1)} %add.94), channel_id=1, source_target_pairs={{0,1},{1,0},{2,3},{3,2},{4,5},{5,4},{6,7},{7,6},{8,9},{9,8},{10,11... | collective-permute-start | bytes 86024 | tf_op jit(solution)/shard_map/ppermute | solution.py:29
  234.9 21.6 %all-to-all-start.3 = ((bf16[16,32,1024]{2,1,0:T(8,128)(2,1)}), bf16[16,32,1024]{2,1,0:T(8,128)(2,1)S(1)}, u32[]{:S(2)}, u32[]{:S(2)}) async-start(bf16[16,32,1024]{2,1,0:T(8,128)(2,1)} %bitcast.26), calls=%async_computation.3 | async-start | bytes 2097152 | tf_op jit(solution)/shard_map/all_to_all | solution.py:428
  (2 other events, 1.3 us)
